TPU v7x, 256 devices: a whole 4x4x8 slice. The times are simulated.
256 devices in a mesh: lon: 32 (over x, y, core), lat: 8 (over z).
Axes of the slice: x: 4, y: 4, z: 8, core: 2. Of those that a mesh axis runs over, the one named last changes fastest.
Arguments:
- surface_forcing: float32 [192, 4096], P('lat', 'lon'), may hold values from -33 to 33
- sea_mask: int32 [192, 4096], P('lat', 'lon'), may hold values 0 or 1
- level_count: int32 [192, 4096], P('lat', 'lon'), may hold values from 1 to 40
- state: float32 [4, 40, 192, 4096], P(None, None, 'lat', 'lon'), may hold values from -6 to 6
Outputs:
- surface_height: float32 [192, 4096], P('lat', 'lon')
- residual: float32 [192, 4096], P('lat', 'lon')
- tendency: float32 [4, 40, 192, 4096], P(None, None, 'lat', 'lon')
All inputs are finite; a program needn't handle non-finite values. No bound on the sum of `sea_mask` on one device may be relied on, other than what follows from the above.
Results may differ from a plain program's by a relative error of at most 0.0003.
Values sent between devices are 32-bit elements; how exact they have to be, the bound alone decides.
A program may use at most 64 MiB of HBM per device.

v0:
```python
import jax
import jax.numpy as jnp
from jax import lax
from jax.sharding import Mesh
from jax.sharding import PartitionSpec as P

LEV = 40
ITERS = 4
LON = ("lon_0", "lon_1", "lon_2")


damping = 0.05
face_scale = 1.0
viscosity = 0.02


def copy_for_each(array, axis):
    copies = jnp.broadcast_to(array, (lax.axis_size(axis), *array.shape))
    return lax.all_to_all(copies, axis, split_axis=0, concat_axis=0, tiled=True)


def of_everyone(array, axis):
    everything = copy_for_each(array, axis)
    return jnp.sum(everything, axis=0)


def one_axis_at_a_time(array, axes):
    far, near = axes
    nearer = of_everyone(array, near)
    return of_everyone(nearer, far)


def in_one(arrays, axis):
    line, at, gathered = (jnp.concatenate([a.reshape(-1) for a in arrays]), 0, [])
    subtotal = one_axis_at_a_time(line, axis)
    for a in arrays:
        gathered.append(subtotal[at : at + a.size].reshape(a.shape))
        at += a.size
    return tuple(gathered)


def with_halo(cells, sides, width):
    for axis, dim in sides:
        count = lax.axis_size(axis)
        head = lax.slice_in_dim(cells, 0, width, axis=dim)
        tail = lax.slice_in_dim(cells, cells.shape[dim] - width, cells.shape[dim], axis=dim)
        cells = jnp.concatenate(
            [
                lax.ppermute(tail, axis, [(i, (i + 1) % count) for i in range(count)]),
                cells,
                lax.ppermute(head, axis, [((i + 1) % count, i) for i in range(count)]),
            ],
            axis=dim,
        )
    return cells


def trim_rims(field, margin):
    return field[..., margin : field.shape[-2] - margin, margin : field.shape[-1] - margin]


def face_coeffs(depth, width_out, width_in):
    offset = width_in - width_out
    height = depth.shape[0] - 2 * offset
    breadth = depth.shape[1] - 2 * offset
    center = depth[offset : offset + height, offset : offset + breadth]
    east_face = face_scale * jnp.minimum(
        center, depth[offset : offset + height, offset + 1 : offset + 1 + breadth]
    )
    west_face = face_scale * jnp.minimum(
        center, depth[offset : offset + height, offset - 1 : offset - 1 + breadth]
    )
    north_face = face_scale * jnp.minimum(
        center, depth[offset + 1 : offset + 1 + height, offset : offset + breadth]
    )
    south_face = face_scale * jnp.minimum(
        center, depth[offset - 1 : offset - 1 + height, offset : offset + breadth]
    )
    diagonal = damping + east_face + west_face + north_face + south_face
    return (diagonal, east_face, west_face, north_face, south_face)


def operator_apply(padded, coeffs):
    diagonal, east_face, west_face, north_face, south_face = coeffs
    return (
        diagonal * padded[1:-1, 1:-1]
        - east_face * padded[1:-1, 2:]
        - west_face * padded[1:-1, :-2]
        - north_face * padded[2:, 1:-1]
        - south_face * padded[:-2, 1:-1]
    )


def laplace(field, active):
    center = field[..., 1:-1, 1:-1]
    active_center = active[..., 1:-1, 1:-1]
    east_part = active_center * active[..., 1:-1, 2:] * (field[..., 1:-1, 2:] - center)
    west_part = active_center * active[..., 1:-1, :-2] * (center - field[..., 1:-1, :-2])
    north_part = active_center * active[..., 2:, 1:-1] * (field[..., 2:, 1:-1] - center)
    south_part = active_center * active[..., :-2, 1:-1] * (center - field[..., :-2, 1:-1])
    return east_part - west_part + north_part - south_part


def advect(field, active):
    east_flow = field[2]
    north_flow = field[3]
    center = field[..., 1:-1, 1:-1]
    active_center = active[..., 1:-1, 1:-1]
    flow_center = east_flow[..., 1:-1, 1:-1]
    lift_center = north_flow[..., 1:-1, 1:-1]
    east_speed = (
        0.25 * active_center * active[..., 1:-1, 2:] * (flow_center + east_flow[..., 1:-1, 2:])
    )
    west_speed = (
        0.25 * active_center * active[..., 1:-1, :-2] * (flow_center + east_flow[..., 1:-1, :-2])
    )
    north_speed = (
        0.25 * active_center * active[..., 2:, 1:-1] * (lift_center + north_flow[..., 2:, 1:-1])
    )
    south_speed = (
        0.25 * active_center * active[..., :-2, 1:-1] * (lift_center + north_flow[..., :-2, 1:-1])
    )
    return (
        east_speed * (center + field[..., 1:-1, 2:])
        - west_speed * (center + field[..., 1:-1, :-2])
        + north_speed * (center + field[..., 2:, 1:-1])
        - south_speed * (center + field[..., :-2, 1:-1])
    )


def tendency_of(state_wide, active_wide):
    inner_active = trim_rims(active_wide, 1)
    smoothed = laplace(laplace(state_wide, active_wide), inner_active)
    flux = advect(trim_rims(state_wide, 1), inner_active)
    return trim_rims(active_wide, 2) * (-flux - viscosity * smoothed)


def apply_operator(field, width, coeff_list):
    return (operator_apply(field, coeff_list[width - 1]), width - 1)


def paired_totals(residual, search, image, width):
    return in_one(
        (jnp.sum(trim_rims(residual * search, width)), jnp.sum(trim_rims(image * search, width))),
        (("lon_0", "lon_1"), ("lon_2", "lat")),
    )


def paired_solve(forcing, width, coeff_list):
    residual = forcing
    search = residual / coeff_list[width][0]
    image, narrow = apply_operator(search, width, coeff_list)
    residual = trim_rims(residual, width - narrow)
    search = trim_rims(search, width - narrow)
    width = narrow
    product, curvature = paired_totals(residual, search, image, width)
    alpha_step = product / curvature
    direction = search
    along = image
    solution = jnp.zeros_like(residual)
    for step_index in range(ITERS):
        solution = solution + alpha_step * direction
        residual = residual - alpha_step * along
        if step_index + 1 < ITERS:
            search = residual / coeff_list[width][0]
            image, narrow = apply_operator(search, width, coeff_list)
            margin = width - narrow
            residual = trim_rims(residual, margin)
            search = trim_rims(search, margin)
            solution = trim_rims(solution, margin)
            direction = trim_rims(direction, margin)
            along = trim_rims(along, margin)
            width = narrow
            product_next, curvature = paired_totals(residual, search, image, width)
            beta_step = product_next / product
            alpha_step = product_next / (curvature - beta_step * product_next / alpha_step)
            product = product_next
            direction = search + beta_step * direction
            along = image + beta_step * along
    return (solution, residual)


def per_device(surface_forcing, sea_mask, level_count, state):
    height = surface_forcing.shape[0]
    rim_width = ITERS + 1
    columns = jnp.stack([sea_mask, level_count])
    columns_wide = with_halo(columns, ((LON, 2), ("lat", 1)), rim_width)
    rows_global = (
        lax.axis_index("lat") * height
        + jnp.arange(height + 2 * rim_width, dtype=jnp.int32)
        - rim_width
    )
    inside = ((rows_global >= 0) & (rows_global < height * lax.axis_size("lat"))).astype(
        jnp.float32
    )
    sea_wide = columns_wide[0].astype(jnp.float32) * inside[:, None]
    depth = sea_wide * columns_wide[1].astype(jnp.float32) / LEV
    coeff_list = [face_coeffs(depth, width, rim_width) for width in range(rim_width)]
    forcing_wide = with_halo(surface_forcing, ((LON, 1), ("lat", 0)), ITERS)
    forcing = trim_rims(sea_wide, rim_width - ITERS) * forcing_wide
    start_width = ITERS
    solution, residual = paired_solve(forcing, start_width, coeff_list)
    level_index = jnp.arange(state.shape[1], dtype=jnp.int32)[:, None, None]
    sea_near = trim_rims(sea_wide, rim_width - 2)
    count_near = trim_rims(columns_wide[1], rim_width - 2)
    active_wide = (level_index < count_near[None]).astype(jnp.float32) * sea_near[None]
    state_wide = with_halo(state, ((LON, 3), ("lat", 2)), 2)
    tendency = tendency_of(state_wide, active_wide)
    return (solution, residual, tendency)


def solution(mesh):
    finer = Mesh(
        mesh.devices.reshape(4, 4, 2, mesh.shape["lat"]), ("lon_0", "lon_1", "lon_2", "lat")
    )
    in_specs = (P("lat", LON), P("lat", LON), P("lat", LON), P(None, None, "lat", LON))
    out_specs = (P("lat", LON), P("lat", LON), P(None, None, "lat", LON))
    return jax.shard_map(
        per_device, mesh=finer, in_specs=in_specs, out_specs=out_specs, check_vma=False
    )
```

profile of v0, /device:TPU:1, one launch (start us, length us, event | category | flops | bytes accessed | tf_op | source)
XLA Modules:
  0.0 201.9 jit_solution(4381668178346828135)
XLA Ops:
  0.6 0.9 fusion.82
  1.5 2.7 %collective-permute-start.4 = (f32[24,4]{1,0:T(8,128)S(1)}, f32[24,4]{1,0:T(8,128)S(1)}, u32[]{:S(2)}, u32[]{:S(2)}) collective-permute-start(f32[24,4]{1,0:T(8,128)S(1)} %get-tuple-element.68), channel_id=1, source_target_pairs={{0,8},{8,16},{16,24},{24,32},{32,40},{40,48},{48,56},{56,64},{64,7... | collective-permute-start | bytes 1160 | tf_op jit(solution)/shard_map/ppermute | solution.py:49
  4.7 0.9 slice_add_fusion.4
  5.6 1.2 collective-permute-start
  6.8 3.9 %collective-permute-start.1 = (s32[2,24,5]{2,1,0:T(8,128)S(1)}, s32[2,24,5]{2,1,0:T(8,128)S(1)}, u32[]{:S(2)}, u32[]{:S(2)}) collective-permute-start(s32[2,24,5]{2,1,0:T(8,128)S(1)} %get-tuple-element.67), channel_id=1, source_target_pairs={{8,0},{16,8},{24,16},{32,24},{40,32},{48,40},{56,48},{64,56},{72,6... | collective-permute-start | bytes 2888 | tf_op jit(solution)/shard_map/ppermute | solution.py:51
  10.7 0.6 collective-permute-done
  11.6 0.8 pad_add_fusion.5
  12.6 4.0 %collective-permute-start.3 = (s32[2,5,138]{2,1,0:T(8,128)S(1)}, s32[2,5,138]{2,1,0:T(8,128)S(1)}, u32[]{:S(2)}, u32[]{:S(2)}) collective-permute-start(s32[2,5,138]{2,1,0:T(8,128)S(1)} %get-tuple-element.53), channel_id=1, source_target_pairs={{1,0},{2,1},{3,2},{4,3},{5,4},{6,5},{7,6},{0,7},{9,8},{10,9},{11,1... | collective-permute-start | bytes 16568 | tf_op jit(solution)/shard_map/ppermute | solution.py:51
  16.6 0.8 pad_maximum_fusion.14
  17.4 2.7 %collective-permute-start.7 = (f32[4,136]{1,0:T(4,128)S(1)}, f32[4,136]{1,0:T(4,128)S(1)}, u32[]{:S(2)}, u32[]{:S(2)}) collective-permute-start(f32[4,136]{1,0:T(4,128)S(1)} %get-tuple-element.57), channel_id=1, source_target_pairs={{1,0},{2,1},{3,2},{4,3},{5,4},{6,5},{7,6},{0,7},{9,8},{10,9},{11,1... | collective-permute-start | bytes 6536 | tf_op jit(solution)/shard_map/ppermute | solution.py:51
  20.1 0.8 pad_add_fusion
  21.1 0.8 fusion.52
  22.2 0.7 fusion.74
  22.8 1.4 pad_maximum_fusion.15
  24.2 20.0 %all_to_all.48 = f32[16,1,2]{2,1,0:T(1,128)S(1)} all-to-all(f32[16,1,2]{2,1,0:T(1,128)S(1)} %broadcast_in_dim.16), channel_id=1, replica_groups=mesh['lon_0'=4,'lon_1'=4,'lon_2'=2,'lat'=8] {'lon_2','lat'}, dimensions={0} | all-to-all | bytes 256 | tf_op jit(solution)/shard_map/all_to_all | solution.py:19
  44.3 0.6 broadcast_in_dim.17
  44.9 4.2 %all-to-all-start.1 = ((f32[16,1,2]{2,1,0:T(1,128)}), f32[16,1,2]{2,1,0:T(1,128)S(1)}, u32[]{:S(2)}, u32[]{:S(2)}) async-start(f32[16,1,2]{2,1,0:T(1,128)} %broadcast_in_dim.17), calls=%async_computation.1 | async-start | bytes 16384 | tf_op jit(solution)/shard_map/all_to_all | solution.py:19
  49.0 4.0 %fusion.79 = (f32[4,40,24,2]{3,2,1,0:T(8,128)S(1)}, f32[4,40,24,2]{3,2,1,0:T(8,128)}) fusion(f32[4,40,24,128]{3,2,1,0:T(8,128)} %param.7), kind=kLoop, calls=%fused_computation.186 | loop fusion | bytes 122880 | tf_op jit(solution)/shard_map/slice | solution.py:46
  53.1 2.3 %all-to-all-done.1 = f32[16,1,2]{2,1,0:T(1,128)S(1)} async-done(((f32[16,1,2]{2,1,0:T(1,128)}), f32[16,1,2]{2,1,0:T(1,128)S(1)}, u32[]{:S(2)}, u32[]{:S(2)}) %all-to-all-start.1) | async-done | bytes 160 | tf_op jit(solution)/shard_map/all_to_all | solution.py:19
  55.4 0.6 fusion.86
  57.7 0.7 fusion.72
  58.4 1.3 pad_maximum_fusion.16
  59.7 0.6 broadcast_in_dim.18
  60.3 5.4 %all-to-all-start.2 = ((f32[16,1,2]{2,1,0:T(1,128)}), f32[16,1,2]{2,1,0:T(1,128)S(1)}, u32[]{:S(2)}, u32[]{:S(2)}) async-start(f32[16,1,2]{2,1,0:T(1,128)} %broadcast_in_dim.18), calls=%async_computation.2 | async-start | bytes 16384 | tf_op jit(solution)/shard_map/all_to_all | solution.py:19
  65.7 2.9 %copy.74 = f32[4,40,24,2]{1,2,3,0:T(8,128)} copy(f32[4,40,24,2]{3,2,1,0:T(8,128)} %get-tuple-element.40) | data formatting | bytes 61440
  68.8 1.4 copy.73
  70.2 2.4 %all-to-all-done.2 = f32[16,1,2]{2,1,0:T(1,128)S(1)} async-done(((f32[16,1,2]{2,1,0:T(1,128)}), f32[16,1,2]{2,1,0:T(1,128)S(1)}, u32[]{:S(2)}, u32[]{:S(2)}) %all-to-all-start.2) | async-done | bytes 160 | tf_op jit(solution)/shard_map/all_to_all | solution.py:19
  72.7 0.6 broadcast_in_dim.19
  73.3 3.5 %all-to-all-start.3 = ((f32[16,1,2]{2,1,0:T(1,128)}), f32[16,1,2]{2,1,0:T(1,128)S(1)}, u32[]{:S(2)}, u32[]{:S(2)}) async-start(f32[16,1,2]{2,1,0:T(1,128)} %broadcast_in_dim.19), calls=%async_computation.3 | async-start | bytes 16384 | tf_op jit(solution)/shard_map/all_to_all | solution.py:19
  76.7 2.5 %collective-permute-start.8 = (f32[4,40,24,2]{1,2,3,0:T(8,128)}, f32[4,40,24,2]{1,2,3,0:T(8,128)}, u32[]{:S(2)}, u32[]{:S(2)}) collective-permute-start(f32[4,40,24,2]{1,2,3,0:T(8,128)} %copy.73), channel_id=1, source_target_pairs={{0,8},{8,16},{16,24},{24,32},{32,40},{40,48},{48,56},{56,64},{64,7... | collective-permute-start | bytes 92168 | tf_op jit(solution)/shard_map/ppermute | solution.py:49
  79.3 1.9 copy.46
  81.1 1.9 all-to-all-done.3
  88.4 0.7 fusion.70
  89.1 1.4 pad_maximum_fusion.17
  90.5 0.6 broadcast_in_dim.20
  91.1 7.2 %all-to-all-start.4 = ((f32[16,1,2]{2,1,0:T(1,128)}), f32[16,1,2]{2,1,0:T(1,128)S(1)}, u32[]{:S(2)}, u32[]{:S(2)}) async-start(f32[16,1,2]{2,1,0:T(1,128)} %broadcast_in_dim.20), calls=%async_computation.4 | async-start | bytes 16384 | tf_op jit(solution)/shard_map/all_to_all | solution.py:19
  98.5 6.8 %all-to-all-done.4 = f32[16,1,2]{2,1,0:T(1,128)S(1)} async-done(((f32[16,1,2]{2,1,0:T(1,128)}), f32[16,1,2]{2,1,0:T(1,128)S(1)}, u32[]{:S(2)}, u32[]{:S(2)}) %all-to-all-start.4) | async-done | bytes 160 | tf_op jit(solution)/shard_map/all_to_all | solution.py:19
  105.3 0.6 broadcast_in_dim.21
  105.9 3.5 %all-to-all-start.5 = ((f32[16,1,2]{2,1,0:T(1,128)}), f32[16,1,2]{2,1,0:T(1,128)S(1)}, u32[]{:S(2)}, u32[]{:S(2)}) async-start(f32[16,1,2]{2,1,0:T(1,128)} %broadcast_in_dim.21), calls=%async_computation.5 | async-start | bytes 16384 | tf_op jit(solution)/shard_map/all_to_all | solution.py:19
  109.5 6.2 %all-to-all-done.5 = f32[16,1,2]{2,1,0:T(1,128)S(1)} async-done(((f32[16,1,2]{2,1,0:T(1,128)}), f32[16,1,2]{2,1,0:T(1,128)S(1)}, u32[]{:S(2)}, u32[]{:S(2)}) %all-to-all-start.5) | async-done | bytes 160 | tf_op jit(solution)/shard_map/all_to_all | solution.py:19
  120.1 1.3 multiply_reduce_fusion.1
  121.4 1.4 pad_maximum_fusion.18
  122.8 0.6 broadcast_in_dim.22
  123.4 5.2 %all-to-all-start.6 = ((f32[16,1,2]{2,1,0:T(1,128)}), f32[16,1,2]{2,1,0:T(1,128)S(1)}, u32[]{:S(2)}, u32[]{:S(2)}) async-start(f32[16,1,2]{2,1,0:T(1,128)} %broadcast_in_dim.22), calls=%async_computation.6 | async-start | bytes 16384 | tf_op jit(solution)/shard_map/all_to_all | solution.py:19
  128.6 3.2 %slice_multiply_fusion.3 = (f32[40,26,130]{2,0,1:T(8,128)}, f32[40,26,130]{2,0,1:T(8,128)}, f32[40,26,130]{2,0,1:T(8,128)}, f32[40,26,130]{2,0,1:T(8,128)}) fusion(f32[40,28,132]{2,0,1:T(8,128)S(1)} %fusion.29), kind=kLoop, calls=%fused_computation.51 | loop fusion | flops 540800 | bytes 4867200 | tf_op jit(solution)/shard_map/mul | solution.py:97
  131.8 3.6 %all-to-all-done.6 = f32[16,1,2]{2,1,0:T(1,128)S(1)} async-done(((f32[16,1,2]{2,1,0:T(1,128)}), f32[16,1,2]{2,1,0:T(1,128)S(1)}, u32[]{:S(2)}, u32[]{:S(2)}) %all-to-all-start.6) | async-done | bytes 160 | tf_op jit(solution)/shard_map/all_to_all | solution.py:19
  135.5 0.6 broadcast_in_dim.23
  136.1 3.5 %all-to-all-start.7 = ((f32[16,1,2]{2,1,0:T(1,128)}), f32[16,1,2]{2,1,0:T(1,128)S(1)}, u32[]{:S(2)}, u32[]{:S(2)}) async-start(f32[16,1,2]{2,1,0:T(1,128)} %broadcast_in_dim.23), calls=%async_computation.7 | async-start | bytes 16384 | tf_op jit(solution)/shard_map/all_to_all | solution.py:19
  139.7 6.2 %all-to-all-done.7 = f32[16,1,2]{2,1,0:T(1,128)S(1)} async-done(((f32[16,1,2]{2,1,0:T(1,128)}), f32[16,1,2]{2,1,0:T(1,128)S(1)}, u32[]{:S(2)}, u32[]{:S(2)}) %all-to-all-start.7) | async-done | bytes 160 | tf_op jit(solution)/shard_map/all_to_all | solution.py:19
  150.4 0.7 fusion.68
  151.0 2.9 %copy.45 = f32[4,40,24,2]{3,1,2,0:T(8,128)} copy(f32[4,40,24,2]{1,2,3,0:T(8,128)} %collective-permute-done.8) | data formatting | bytes 61440 | tf_op jit(solution)/shard_map/ppermute | solution.py:49
  153.9 2.9 %copy.47 = f32[4,40,24,2]{3,1,2,0:T(8,128)} copy(f32[4,40,24,2]{1,2,3,0:T(8,128)} %collective-permute-done.9) | data formatting | bytes 61440 | tf_op jit(solution)/shard_map/ppermute | solution.py:51
  156.8 1.6 pad_maximum_fusion.9
  158.9 1.1 collective-permute-start.10
  160.0 0.7 fusion.61
  160.7 5.3 %collective-permute-done.11 = f32[4,40,2,132]{3,1,2,0:T(8,128)S(1)} collective-permute-done((f32[4,40,2,132]{3,1,2,0:T(8,128)S(1)}, f32[4,40,2,132]{3,1,2,0:T(8,128)S(1)}, u32[]{:S(2)}, u32[]{:S(2)}) %collective-permute-start.11) | collective-permute-done | bytes 168992 | tf_op jit(solution)/shard_map/ppermute | solution.py:51
  165.9 1.3 collective-permute-done.10
  167.3 2.1 %pad_maximum_fusion = f32[4,40,28,132]{3,1,2,0:T(8,128)S(1)} fusion(f32[4,40,2,132]{3,1,2,0:T(8,128)S(1)} %collective-permute-done.11, f32[4,40,24,2]{3,1,2,0:T(8,128)S(1)} %copy-done.2, f32[4,40,24,128]{3,1,2,0:T(8,128)S(1)} %copy.46, f32[4,40,24,2]{3,1,2,0:T(8,128)S(1)} %copy-done, f32[4,40,2,132]{3,1,2,0:T(8,128)S(1)} %collective-permute-done.10), kind=kLoop, calls=%fused_computation | loop fusion | flops 2365440 | bytes 4730880 | tf_op jit(solution)/shard_map/concatenate | solution.py:47
  169.3 0.6 slice_bitcast_fusion.1
  170.0 1.6 fusion.33
  171.6 2.9 %fusion.80 = (f32[40,24,128]{2,0,1:T(8,128)}, f32[40,24,128]{2,0,1:T(8,128)}, f32[40,24,128]{2,0,1:T(8,128)}, f32[40,24,128]{2,0,1:T(8,128)}, f32[40,24,128]{2,0...) fusion(f32[40,28,132]{2,0,1:T(8,128)S(1)} %fusion.29, f32[40,26,130]{2,0,1:T(8,128)S(1)} %get-tuple-element.34), kind=kLoop, calls=%fused_computation.187 | loop fusion | flops 1351680 | bytes 7372800 | tf_op jit(solution)/shard_map/slice | solution.py:59
  174.5 11.8 %fusion.2 = f32[4,40,26,130]{3,1,2,0:T(8,128)} fusion(f32[4,40,2,132]{3,1,2,0:T(8,128)S(1)} %collective-permute-done.10, f32[4,40,24,2]{3,1,2,0:T(8,128)S(1)} %copy-done.2, f32[4,40,24,128]{3,1,2,0:T(8,128)S(1)} %copy.46, f32[4,40,24,2]{3,1,2,0:T(8,128)S(1)} %copy-done, f32[4,40,2,132]{3,1,2,0:T(8,128)S(1)} %collective-permute-done.11, ...), kind=kLoop, calls=%fused_computation.4 | loop fusion | flops 9193600 | bytes 13181440 | tf_op jit(solution)/shard_map/sub | solution.py:101
  186.3 12.5 %fusion.13 = f32[4,40,24,128]{3,1,2,0:T(8,128)} fusion(f32[4,40,26,130]{3,1,2,0:T(8,128)} %fusion.2, f32[4,40,24,128]{3,1,2,0:T(8,128)S(1)} %copy.46, f32[4,40,2,132]{3,1,2,0:T(8,128)} %copy-done.4, f32[4,40,24,2]{3,1,2,0:T(8,128)} %copy.47, f32[4,40,24,2]{3,1,2,0:T(8,128)S(1)} %copy-done.1, f32[4,40,2,132]{3,1,2,0:T(8,128)S(1)} %collective-permute-done.11, ...), kind=kLoop, calls=%fused_computation.23 | loop fusion | flops 16711680 | bytes 18585600 | tf_op jit(solution)/shard_map/mul | solution.py:135
  198.8 3.2 %copy.56 = f32[4,40,24,128]{3,2,1,0:T(8,128)} copy(f32[4,40,24,128]{3,1,2,0:T(8,128)} %fusion.13) | data formatting | bytes 3932160
  (57 shorter events, 5.3 us)
Async XLA Ops:
  1.5 15.1 %collective-permute-start.4 = (f32[24,4]{1,0:T(8,128)S(1)}, f32[24,4]{1,0:T(8,128)S(1)}, u32[]{:S(2)}, u32[]{:S(2)}) collective-permute-start(f32[24,4]{1,0:T(8,128)S(1)} %get-tuple-element.68), channel_id=1, source_target_pairs={{0,8},{8,16},{16,24},{24,32},{32,40},{40,48},{48,56},{56,64},{64,7... | collective-permute-start | bytes 1160 | tf_op jit(solution)/shard_map/ppermute | solution.py:49
  4.2 12.4 %collective-permute-start.5 = (f32[24,4]{1,0:T(8,128)S(1)}, f32[24,4]{1,0:T(8,128)S(1)}, u32[]{:S(2)}, u32[]{:S(2)}) collective-permute-start(f32[24,4]{1,0:T(8,128)S(1)} %get-tuple-element.69), channel_id=1, source_target_pairs={{8,0},{16,8},{24,16},{32,24},{40,32},{48,40},{56,48},{64,56},{72,6... | collective-permute-start | bytes 1160 | tf_op jit(solution)/shard_map/ppermute | solution.py:51
  5.6 5.8 %collective-permute-start = (s32[2,24,5]{2,1,0:T(8,128)S(1)}, s32[2,24,5]{2,1,0:T(8,128)S(1)}, u32[]{:S(2)}, u32[]{:S(2)}) collective-permute-start(s32[2,24,5]{2,1,0:T(8,128)S(1)} %get-tuple-element.66), channel_id=1, source_target_pairs={{0,8},{8,16},{16,24},{24,32},{32,40},{40,48},{48,56},{56,64},{64,7... | collective-permute-start | bytes 2888 | tf_op jit(solution)/shard_map/ppermute | solution.py:49
  6.8 4.8 %collective-permute-start.1 = (s32[2,24,5]{2,1,0:T(8,128)S(1)}, s32[2,24,5]{2,1,0:T(8,128)S(1)}, u32[]{:S(2)}, u32[]{:S(2)}) collective-permute-start(s32[2,24,5]{2,1,0:T(8,128)S(1)} %get-tuple-element.67), channel_id=1, source_target_pairs={{8,0},{16,8},{24,16},{32,24},{40,32},{48,40},{56,48},{64,56},{72,6... | collective-permute-start | bytes 2888 | tf_op jit(solution)/shard_map/ppermute | solution.py:51
  12.4 7.7 %collective-permute-start.2 = (s32[2,5,138]{2,1,0:T(8,128)S(1)}, s32[2,5,138]{2,1,0:T(8,128)S(1)}, u32[]{:S(2)}, u32[]{:S(2)}) collective-permute-start(s32[2,5,138]{2,1,0:T(8,128)S(1)} %get-tuple-element.52), channel_id=1, source_target_pairs={{0,1},{1,2},{2,3},{3,4},{4,5},{5,6},{6,7},{7,0},{8,9},{9,10},{10,1... | collective-permute-start | bytes 16568 | tf_op jit(solution)/shard_map/ppermute | solution.py:49
  12.6 7.5 %collective-permute-start.3 = (s32[2,5,138]{2,1,0:T(8,128)S(1)}, s32[2,5,138]{2,1,0:T(8,128)S(1)}, u32[]{:S(2)}, u32[]{:S(2)}) collective-permute-start(s32[2,5,138]{2,1,0:T(8,128)S(1)} %get-tuple-element.53), channel_id=1, source_target_pairs={{1,0},{2,1},{3,2},{4,3},{5,4},{6,5},{7,6},{0,7},{9,8},{10,9},{11,1... | collective-permute-start | bytes 16568 | tf_op jit(solution)/shard_map/ppermute | solution.py:51
  17.4 3.7 %collective-permute-start.6 = (f32[4,136]{1,0:T(4,128)S(1)}, f32[4,136]{1,0:T(4,128)S(1)}, u32[]{:S(2)}, u32[]{:S(2)}) collective-permute-start(f32[4,136]{1,0:T(4,128)S(1)} %get-tuple-element.56), channel_id=1, source_target_pairs={{0,1},{1,2},{2,3},{3,4},{4,5},{5,6},{6,7},{7,0},{8,9},{9,10},{10,1... | collective-permute-start | bytes 6536 | tf_op jit(solution)/shard_map/ppermute | solution.py:49
  17.4 3.7 %collective-permute-start.7 = (f32[4,136]{1,0:T(4,128)S(1)}, f32[4,136]{1,0:T(4,128)S(1)}, u32[]{:S(2)}, u32[]{:S(2)}) collective-permute-start(f32[4,136]{1,0:T(4,128)S(1)} %get-tuple-element.57), channel_id=1, source_target_pairs={{1,0},{2,1},{3,2},{4,3},{5,4},{6,5},{7,6},{0,7},{9,8},{10,9},{11,1... | collective-permute-start | bytes 6536 | tf_op jit(solution)/shard_map/ppermute | solution.py:51
  44.9 10.5 %all-to-all-start.1 = ((f32[16,1,2]{2,1,0:T(1,128)}), f32[16,1,2]{2,1,0:T(1,128)S(1)}, u32[]{:S(2)}, u32[]{:S(2)}) async-start(f32[16,1,2]{2,1,0:T(1,128)} %broadcast_in_dim.17), calls=%async_computation.1 | async-start | bytes 16384 | tf_op jit(solution)/shard_map/all_to_all | solution.py:19
  60.3 12.3 %all-to-all-start.2 = ((f32[16,1,2]{2,1,0:T(1,128)}), f32[16,1,2]{2,1,0:T(1,128)S(1)}, u32[]{:S(2)}, u32[]{:S(2)}) async-start(f32[16,1,2]{2,1,0:T(1,128)} %broadcast_in_dim.18), calls=%async_computation.2 | async-start | bytes 16384 | tf_op jit(solution)/shard_map/all_to_all | solution.py:19
  68.6 85.3 %collective-permute-start.9 = (f32[4,40,24,2]{1,2,3,0:T(8,128)}, f32[4,40,24,2]{1,2,3,0:T(8,128)}, u32[]{:S(2)}, u32[]{:S(2)}) collective-permute-start(f32[4,40,24,2]{1,2,3,0:T(8,128)} %copy.74), channel_id=1, source_target_pairs={{8,0},{16,8},{24,16},{32,24},{40,32},{48,40},{56,48},{64,56},{72,6... | collective-permute-start | bytes 92168 | tf_op jit(solution)/shard_map/ppermute | solution.py:51
  73.3 9.8 %all-to-all-start.3 = ((f32[16,1,2]{2,1,0:T(1,128)}), f32[16,1,2]{2,1,0:T(1,128)S(1)}, u32[]{:S(2)}, u32[]{:S(2)}) async-start(f32[16,1,2]{2,1,0:T(1,128)} %broadcast_in_dim.19), calls=%async_computation.3 | async-start | bytes 16384 | tf_op jit(solution)/shard_map/all_to_all | solution.py:19
  76.7 74.3 %collective-permute-start.8 = (f32[4,40,24,2]{1,2,3,0:T(8,128)}, f32[4,40,24,2]{1,2,3,0:T(8,128)}, u32[]{:S(2)}, u32[]{:S(2)}) collective-permute-start(f32[4,40,24,2]{1,2,3,0:T(8,128)} %copy.73), channel_id=1, source_target_pairs={{0,8},{8,16},{16,24},{24,32},{32,40},{40,48},{48,56},{56,64},{64,7... | collective-permute-start | bytes 92168 | tf_op jit(solution)/shard_map/ppermute | solution.py:49
  91.1 14.1 %all-to-all-start.4 = ((f32[16,1,2]{2,1,0:T(1,128)}), f32[16,1,2]{2,1,0:T(1,128)S(1)}, u32[]{:S(2)}, u32[]{:S(2)}) async-start(f32[16,1,2]{2,1,0:T(1,128)} %broadcast_in_dim.20), calls=%async_computation.4 | async-start | bytes 16384 | tf_op jit(solution)/shard_map/all_to_all | solution.py:19
  105.9 9.8 %all-to-all-start.5 = ((f32[16,1,2]{2,1,0:T(1,128)}), f32[16,1,2]{2,1,0:T(1,128)S(1)}, u32[]{:S(2)}, u32[]{:S(2)}) async-start(f32[16,1,2]{2,1,0:T(1,128)} %broadcast_in_dim.21), calls=%async_computation.5 | async-start | bytes 16384 | tf_op jit(solution)/shard_map/all_to_all | solution.py:19
  123.4 12.0 %all-to-all-start.6 = ((f32[16,1,2]{2,1,0:T(1,128)}), f32[16,1,2]{2,1,0:T(1,128)S(1)}, u32[]{:S(2)}, u32[]{:S(2)}) async-start(f32[16,1,2]{2,1,0:T(1,128)} %broadcast_in_dim.22), calls=%async_computation.6 | async-start | bytes 16384 | tf_op jit(solution)/shard_map/all_to_all | solution.py:19
  136.1 9.8 %all-to-all-start.7 = ((f32[16,1,2]{2,1,0:T(1,128)}), f32[16,1,2]{2,1,0:T(1,128)S(1)}, u32[]{:S(2)}, u32[]{:S(2)}) async-start(f32[16,1,2]{2,1,0:T(1,128)} %broadcast_in_dim.23), calls=%async_computation.7 | async-start | bytes 16384 | tf_op jit(solution)/shard_map/all_to_all | solution.py:19
  156.8 3.2 %copy-start.6 = (f32[24,128]{1,0:T(8,128)S(1)}, f32[24,128]{1,0:T(8,128)}, u32[]{:S(2)}) copy-start(f32[24,128]{1,0:T(8,128)} %get-tuple-element.20) | copy-start | bytes 36868
  156.8 10.4 %copy-start = (f32[4,40,24,2]{3,1,2,0:T(8,128)S(1)}, f32[4,40,24,2]{3,1,2,0:T(8,128)}, u32[]{:S(2)}) copy-start(f32[4,40,24,2]{3,1,2,0:T(8,128)} %copy.45) | copy-start | bytes 92164
  156.8 10.4 %copy-start.2 = (f32[4,40,24,2]{3,1,2,0:T(8,128)S(1)}, f32[4,40,24,2]{3,1,2,0:T(8,128)}, u32[]{:S(2)}) copy-start(f32[4,40,24,2]{3,1,2,0:T(8,128)} %copy.47) | copy-start | bytes 92164
  158.5 7.5 %collective-permute-start.11 = (f32[4,40,2,132]{3,1,2,0:T(8,128)S(1)}, f32[4,40,2,132]{3,1,2,0:T(8,128)S(1)}, u32[]{:S(2)}, u32[]{:S(2)}) collective-permute-start(f32[4,40,2,132]{3,1,2,0:T(8,128)S(1)} %get-tuple-element.31), channel_id=1, source_target_pairs={{1,0},{2,1},{3,2},{4,3},{5,4},{6,5},{7,6},{0,7},{9,8},{10,9},{11,1... | collective-permute-start | bytes 506888 | tf_op jit(solution)/shard_map/ppermute | solution.py:51
  158.9 8.4 %collective-permute-start.10 = (f32[4,40,2,132]{3,1,2,0:T(8,128)S(1)}, f32[4,40,2,132]{3,1,2,0:T(8,128)S(1)}, u32[]{:S(2)}, u32[]{:S(2)}) collective-permute-start(f32[4,40,2,132]{3,1,2,0:T(8,128)S(1)} %get-tuple-element.32), channel_id=1, source_target_pairs={{0,1},{1,2},{2,3},{3,4},{4,5},{5,6},{6,7},{7,0},{8,9},{9,10},{10,1... | collective-permute-start | bytes 506888 | tf_op jit(solution)/shard_map/ppermute | solution.py:49
  167.3 7.2 %copy-start.4 = (f32[4,40,2,132]{3,1,2,0:T(8,128)}, f32[4,40,2,132]{3,1,2,0:T(8,128)S(1)}, u32[]{:S(2)}) copy-start(f32[4,40,2,132]{3,1,2,0:T(8,128)S(1)} %collective-permute-done.10) | copy-start | bytes 506884
  171.6 2.9 %copy-start.3 = (f32[40,26,130]{2,0,1:T(8,128)S(1)}, f32[40,26,130]{2,0,1:T(8,128)}, u32[]{:S(2)}) copy-start(f32[40,26,130]{2,0,1:T(8,128)} %get-tuple-element.48) | copy-start | bytes 1622404
  174.5 11.8 %copy-start.1 = (f32[4,40,24,2]{3,1,2,0:T(8,128)S(1)}, f32[4,40,24,2]{3,1,2,0:T(8,128)}, u32[]{:S(2)}) copy-start(f32[4,40,24,2]{3,1,2,0:T(8,128)} %copy.45) | copy-start | bytes 92164
  174.5 11.8 %copy-start.5 = (f32[40,24,128]{2,0,1:T(8,128)S(1)}, f32[40,24,128]{2,0,1:T(8,128)}, u32[]{:S(2)}) copy-start(f32[40,24,128]{2,0,1:T(8,128)} %get-tuple-element.41) | copy-start | bytes 1474564
where the time goes:
time: 204 us; the launch traced here: 202 us
  starting transfers between devices  51.9 us (25%)
  other arithmetic  51.2 us (25%)
  waiting for transfers between devices  37.1 us (18%)
  local copies, waits for them, and re-layouts  27.7 us (14%)
  blocking collectives  20 us (10%)
  between operations  14.1 us (7%)
    all_to_all x7, starting transfers between devices, copy_for_each(): return lax.all_to_all(copies, axis, split_axis=0, concat_axis=0, tiled=True)  32.4 us
    all_to_all x7, waiting for transfers between devices, copy_for_each(): return lax.all_to_all(copies, axis, split_axis=0, concat_axis=0, tiled=True)  29.5 us
    all_to_all x1, blocking collectives, copy_for_each(): return lax.all_to_all(copies, axis, split_axis=0, concat_axis=0, tiled=True)  20 us
    mul x1, other arithmetic, tendency_of(): return trim_rims(active_wide, 2) * (-flux - viscosity * smoothed)  12.5 us
    sub x1, other arithmetic, laplace(): return east_part - west_part + north_part - south_part  11.8 us
    ppermute x6, starting transfers between devices, with_halo(): lax.ppermute(head, axis, [((i + 1) % count, i) for i in range(count)])  11.8 us
    unnamed x18, local copies, waits for them, and re-layouts  9.35 us
    ppermute x6, starting transfers between devices, with_halo(): lax.ppermute(tail, axis, [(i, (i + 1) % count) for i in range(count)])  7.72 us
  transfers between devices with their start and end apart: 19, of which 12 were waited for; matrix products, arithmetic and copies ran while one was open for 16% of the time, Pallas kernels for 0%

commit v1 on v0

v1 whole, which is shorter than its diff:
```python
import jax
import jax.numpy as jnp
from jax import lax
from jax.experimental import pallas as pl
from jax.experimental.pallas import tpu as pltpu
from jax.sharding import PartitionSpec as P

MESH = pl.DeviceIdType.MESH
F32 = jnp.float32
CORES = 2
GROUP = 16
VISC = 0.02
DIRS = ((1, 0), (-1, 0), (0, 1), (0, -1), (1, 1), (-1, -1), (1, -1), (-1, 1))
OPP = (1, 0, 3, 2, 5, 4, 7, 6)
E, W, N, S, NE, SW, SE, NW = range(8)


def two_sum(a, b):
    s = a + b
    t = s - a
    return s, (a - (s - t)) + (b - t)


def quick(a, b):
    s = a + b
    return s, b - (s - a)


def split(a):
    t = 4097.0 * a
    h = t - (t - a)
    return h, a - h


def two_prod(a, b):
    p = a * b
    ah, al = split(a)
    bh, bl = split(b)
    return p, ((ah * bh - p) + ah * bl + al * bh) + al * bl


def int_prod(w, h):
    p = w * h
    a, b = split(h)
    return p, (w * a - p) + w * b


def dd_add(a, b):
    s, e = two_sum(a[0], b[0])
    return quick(s, e + (a[1] + b[1]))


def dd_mul(a, b):
    p, e = two_prod(a[0], b[0])
    return quick(p, e + (a[0] * b[1] + a[1] * b[0]))


def dd_neg(a):
    return -a[0], -a[1]


def dd_div(a, b):
    r = 1.0 / b[0]
    q = a[0] * r
    p, e = two_prod(q, b[0])
    rest = ((a[0] - p) - e) + (a[1] - q * b[1])
    return quick(q, rest * r)


def iota(shape, dim):
    return lax.broadcasted_iota(jnp.int32, shape, dim)


def shift_rows(x, step):
    return pltpu.roll(x, (-step) % x.shape[0], 0)


def shift_lanes(x, step):
    return pltpu.roll(x, (-step) % 128, 1)


def cg_coefficients(mu):
    s, t = dict(enumerate(mu)), dict(enumerate(mu))
    one = (jnp.ones_like(mu[0][0]), jnp.zeros_like(mu[0][0]))
    p, q = [one], [one]
    x = []
    for k in range(4):
        alpha = dd_div(s[k], t[k + 1])
        minus = dd_neg(alpha)
        x = [dd_add(x[i], dd_mul(alpha, q[i])) if i < len(x) else dd_mul(alpha, q[i]) for i in range(k + 1)]
        moved = [dd_mul(minus, c) for c in q]
        p = [p[i] if i == 0 else (dd_add(p[i], moved[i - 1]) if i <= k else moved[i - 1]) for i in range(k + 2)]
        if k < 3:
            last = 6 - k
            s_next = {j: dd_add(s[j], dd_mul(minus, t[j + 1])) for j in range(k + 1, last + 1)}
            beta = dd_mul(minus, dd_div(s_next[k + 1], s[k]))
            t = {j: dd_add(s_next[j], dd_mul(beta, t[j])) for j in range(k + 2, last + 1)}
            s = s_next
            q = [dd_add(p[i], dd_mul(beta, q[i])) if i <= k else p[i] for i in range(k + 2)]
    return x, p


def tendencies(active, quads):
    east = shift_lanes(active, 1)
    north = shift_rows(active, 1)
    face_e = active * east
    face_n = active * north
    count = face_e + shift_lanes(face_e, -1) + face_n + shift_rows(face_n, -1)
    u, v = quads[2], quads[3]
    flow_e = (0.25 * face_e) * (u + shift_lanes(u, 1))
    flow_n = (0.25 * face_n) * (v + shift_rows(v, 1))
    own = slice(0, 24)
    flow_w = shift_lanes(flow_e, -1)[own]
    flow_s = shift_rows(flow_n, -1)[own]
    flow_e, flow_n = flow_e[own], flow_n[own]
    net = (flow_e - flow_w) + (flow_n - flow_s)
    out = []
    for q in quads:
        q = active * q
        qe, qw, qn, qs = shift_lanes(q, 1), shift_lanes(q, -1), shift_rows(q, 1), shift_rows(q, -1)
        lap = active * ((qe + qw) + (qn + qs)) - count * q
        around = (shift_lanes(lap, 1) + shift_lanes(lap, -1)) + (shift_rows(lap, 1) + shift_rows(lap, -1))
        flux = (net * q[own] + flow_e * qe[own]) + (flow_n * qn[own] - flow_w * qw[own]) - flow_s * qs[own]
        out.append(VISC * (count[own] * lap[own] - active[own] * around[own]) - flux)
    return out


def make_kernel(nlon, nlat, levels, names):
    nplane = nlon // CORES
    nline = CORES * nlat
    groups = -(-levels // GROUP)
    entries = levels + groups
    order = [names.index("lon"), names.index("lat")]

    def device(lon, lat):
        pair = (lon, lat)
        return (pair[order.index(0)], pair[order.index(1)])

    def kernel(forcing_hbm, sea_hbm, count_hbm, state_hbm, x_ref, r_ref, tend_hbm,
               forcing, sea, count, state, tend, surf, surf_ew, surf_ns, edges, edges_in, rows_up, rows_down,
               rows_in, corners_in, edge_out, partial, gather_a, mid, gather_b,
               in_sem, out_sem, send_sem, recv_sem, send_a, recv_a, send_b, recv_b):
        lon = lax.axis_index("lon")
        lat = lax.axis_index("lat")
        plane, core = lon // CORES, lon % CORES
        line = core * nlat + lat

        small = [pltpu.make_async_copy(a, b, in_sem.at[i]) for i, (a, b) in
                 enumerate(((forcing_hbm, forcing), (sea_hbm, sea), (count_hbm, count)))]
        large = [pltpu.make_async_copy(state_hbm.at[f], state.at[f], in_sem.at[3 + f]) for f in range(4)]
        for copy in small + large:
            copy.start()

        near = [device((lon + dx + nlon) % nlon, (lat + dy + nlat) % nlat) for dx, dy in DIRS]
        plane_peer = [device(((plane + j) % nplane) * CORES + core, lat) for j in range(1, nplane)]
        line_peer = []
        for j in range(1, nline):
            other = (line + j) % nline
            line_peer.append(device(plane * CORES + other // nlat, other % nlat))
        barrier = pltpu.get_barrier_semaphore()
        peers = near + plane_peer + line_peer
        for peer in peers:
            pl.semaphore_signal(barrier, inc=1, device_id=peer, device_id_type=MESH)

        lane = iota((8, 128), 1)
        sub = iota((8, 128), 0)

        for copy in small:
            copy.wait()
        wet = sea[...] * count[...]
        for t in range(3):
            rows = slice(8 * t, 8 * t + 8)
            surf[t, 0] = wet[rows].astype(F32)
            surf[t, 1] = (sea[rows].astype(F32) * forcing[rows]) * 65536.0

        for copy in large:
            copy.wait()

        lane24 = iota((24, 128), 1)

        def pack_edges(f, carry):
            for g in range(groups):
                packed = jnp.zeros((24, 128), F32)
                for i in range(min(GROUP, levels - g * GROUP)):
                    moved = pltpu.roll(state[f, g * GROUP + i], (4 + 8 * i) % 128, 1)
                    packed = jnp.where(lane24 // 8 == i, moved, packed)
                edges[f, g] = packed
            return carry

        lax.fori_loop(0, 4, pack_edges, 0)

        def packed_rows(tile_of):
            up, down = None, None
            for f in range(4):
                top = pltpu.roll(tile_of(f, slice(16, 24)), (2 * f + 2) % 8, 0)
                low = tile_of(f, slice(0, 8))
                low = pltpu.roll(low, 2 * f, 0) if f else low
                up = top if f == 0 else jnp.where(sub // 2 == f, top, up)
                down = low if f == 0 else jnp.where(sub // 2 == f, low, down)
            return up, down

        def pack_rows(k, carry):
            up, down = packed_rows(lambda f, rows: state[f, k, rows])
            rows_up[k] = up
            rows_down[k] = down
            return carry

        lax.fori_loop(0, levels, pack_rows, 0)
        for g in range(groups):
            up, down = packed_rows(lambda f, rows: edges[f, g, rows])
            rows_up[levels + g] = up
            rows_down[levels + g] = down

        pl.semaphore_wait(barrier, len(peers))

        def surf_slot(d):
            return surf_ew.at[d] if d < 2 else surf_ns.at[d - 2]

        def surf_copy(d):
            source = surf if d < 2 else surf.at[2 if DIRS[d][1] > 0 else 0]
            return pltpu.make_async_remote_copy(source, surf_slot(OPP[d]), send_sem.at[d], recv_sem.at[OPP[d]],
                                                device_id=near[d], device_id_type=MESH)

        def rows_copy(d):
            source = rows_up if DIRS[d][1] > 0 else rows_down
            if d < 4:
                target = rows_in.at[OPP[d] - 2]
            else:
                source, target = source.at[pl.ds(levels, groups)], corners_in.at[OPP[d] - 4]
            return pltpu.make_async_remote_copy(source, target, send_sem.at[8 + d], recv_sem.at[8 + OPP[d]],
                                                device_id=near[d], device_id_type=MESH)

        def edge_copy(d):
            return pltpu.make_async_remote_copy(edges, edges_in.at[OPP[d]], send_sem.at[8 + d], recv_sem.at[8 + OPP[d]],
                                                device_id=near[d], device_id_type=MESH)

        surf_copies = [surf_copy(d) for d in range(8)]
        other_copies = [edge_copy(d) if d < 2 else rows_copy(d) for d in range(8)]
        for copy in surf_copies + other_copies:
            copy.start()
        for copy in surf_copies:
            copy.wait_recv()

        has_north = jnp.where(lat < nlat - 1, 1.0, 0.0).astype(F32)
        has_south = jnp.where(lat > 0, 1.0, 0.0).astype(F32)

        def wide(v):
            own = [surf[t, v] for t in range(3)] + [surf_ns[N - 2, v] * has_north, surf_ns[S - 2, v] * has_south]
            side = [jnp.where(lane < 64, surf_ew[E, t, v], surf_ew[W, t, v]) for t in range(3)]
            side.append(jnp.where(lane < 64, surf_ns[NE - 2, v], surf_ns[NW - 2, v]) * has_north)
            side.append(jnp.where(lane < 64, surf_ns[SE - 2, v], surf_ns[SW - 2, v]) * has_south)
            return jnp.concatenate(own, 0), jnp.concatenate(side, 0)

        lane40 = iota((40, 128), 1)

        def to_east(pair):
            a, b = shift_lanes(pair[0], 1), shift_lanes(pair[1], 1)
            return jnp.where(lane40 == 127, b, a), jnp.where(lane40 == 127, a, b)

        def to_west(pair):
            a, b = shift_lanes(pair[0], -1), shift_lanes(pair[1], -1)
            return jnp.where(lane40 == 0, b, a), jnp.where(lane40 == 0, a, b)

        def to_north(pair):
            return shift_rows(pair[0], 1), shift_rows(pair[1], 1)

        def to_south(pair):
            return shift_rows(pair[0], -1), shift_rows(pair[1], -1)

        moves = (to_east, to_west, to_north, to_south)
        depth = wide(0)
        force = wide(1)
        moved = [move(depth) for move in moves]
        faces = [[jnp.minimum(depth[t], m[t]) for m in moved] for t in range(2)]
        diag = [2.0 + ((faces[t][0] + faces[t][1]) + (faces[t][2] + faces[t][3])) for t in range(2)]
        inverse = [1.0 / diag[t] for t in range(2)]

        def over_diag(hi, lo, t):
            q = hi * inverse[t]
            a, b = split(q)
            rest = ((hi - diag[t] * a) - diag[t] * b) + lo
            return q, rest * inverse[t]

        vectors = [[quick(*over_diag(force[t], jnp.zeros_like(force[t]), t)) for t in range(2)]]
        for k in range(4):
            last = vectors[-1]
            high = [move((last[0][0], last[1][0])) for move in moves]
            low = [move((last[0][1], last[1][1])) for move in moves]
            following = []
            for t in range(2):
                if k == 3 and t == 1:
                    continue
                terms = [int_prod(faces[t][i], high[i][t]) for i in range(4)]
                fine = [faces[t][i] * low[i][t] + terms[i][1] for i in range(4)]
                s0, e0 = two_sum(terms[0][0], terms[1][0])
                s1, e1 = two_sum(terms[2][0], terms[3][0])
                s, e2 = two_sum(s0, s1)
                rest = ((e0 + e1) + e2) + ((fine[0] + fine[1]) + (fine[2] + fine[3]))
                q, q_low = over_diag(s, rest, t)
                s, e = two_sum(last[t][0], -q)
                following.append(quick(s, e + (last[t][1] - q_low)))
            vectors.append(following)
        own_vectors = [(v[0][0][:24], v[0][1][:24]) for v in vectors]
        own_diag = diag[0][:24]

        sums = []
        for n in range(8):
            a, b = own_vectors[n // 2], own_vectors[n - n // 2]
            p, e = int_prod(own_diag, a[0])
            product = dd_mul(quick(p, e + own_diag * a[1]), b)
            tiles = [(product[0][8 * i:8 * i + 8], product[1][8 * i:8 * i + 8]) for i in range(3)]
            sums.append(dd_add(dd_add(tiles[0], tiles[1]), tiles[2]))

        def fold(a, b, near_mask, step):
            def one(i):
                x, y = a[i], b[i]
                far = jnp.where(near_mask, pltpu.roll(x, 8 - step, 0), pltpu.roll(y, step, 0))
                return jnp.where(near_mask, x, y), far
            kept, far = zip(*(one(i) for i in range(2)))
            return dd_add(kept, far)

        level = [fold(sums[2 * i], sums[2 * i + 1], sub < 4, 4) for i in range(4)]
        level = [fold(level[2 * i], level[2 * i + 1], sub % 4 < 2, 2) for i in range(2)]
        level = fold(level[0], level[1], sub % 2 < 1, 1)
        far = (pltpu.roll(level[0], 64, 1), pltpu.roll(level[1], 64, 1))
        level = dd_add(level, far)
        partial[...] = jnp.where(lane < 64, level[0], level[1])

        copies_a = [pltpu.make_async_remote_copy(partial, gather_a.at[j], send_a.at[j], recv_a.at[j],
                                                 device_id=plane_peer[j], device_id_type=MESH)
                    for j in range(nplane - 1)]
        for copy in copies_a:
            copy.start()

        def unpacked(message):
            return message, pltpu.roll(message, 64, 1)

        def total(messages):
            parts = [unpacked(m) for m in messages]
            while len(parts) > 1:
                parts = [dd_add(parts[i], parts[i + 1]) if i + 1 < len(parts) else parts[i]
                         for i in range(0, len(parts), 2)]
            return parts[0]

        for d in (N, S):
            other_copies[d].wait_recv()
        count_own = jnp.concatenate([depth[0][:24], jnp.where(sub < 4, depth[0][24:32], depth[0][32:40])], 0)
        count_side = jnp.concatenate([depth[1][:24], jnp.where(sub < 4, depth[1][24:32], depth[1][32:40])], 0)

        def with_rows(f, block, north, south):
            up = pltpu.roll(north, (8 - 2 * f) % 8, 0) if f else north
            down = pltpu.roll(south, 6 - 2 * f, 0) if f < 3 else south
            return jnp.concatenate([block, jnp.where(sub < 4, up, down)], 0)

        def main(k, carry):
            active = jnp.where(count_own > k.astype(F32), 1.0, 0.0)
            north, south = rows_in[N - 2, k], rows_in[S - 2, k]
            quads = [with_rows(f, state[f, k], north, south) for f in range(4)]
            for f, value in enumerate(tendencies(active, quads)):
                tend[f, k] = value
            return carry

        lax.fori_loop(0, levels, main, 0)

        for copy in copies_a:
            copy.wait_recv()
        hi, lo = total([partial[...]] + [gather_a[j] for j in range(nplane - 1)])
        mid[...] = jnp.where(lane < 64, hi, pltpu.roll(lo, 64, 1))
        copies_b = [pltpu.make_async_remote_copy(mid, gather_b.at[j], send_b.at[j], recv_b.at[j],
                                                 device_id=line_peer[j], device_id_type=MESH)
                    for j in range(nline - 1)]
        for copy in copies_b:
            copy.start()

        for d in (E, W, NE, SW, SE, NW):
            other_copies[d].wait_recv()
        lane32 = iota((32, 128), 1)
        left32, left24, left8 = lane32 % 8 < 4, lane24 % 8 < 4, lane % 8 < 4

        def spread(first, second):
            x = jnp.where(lane32 < 8, jnp.where(lane32 < 4, pltpu.roll(first, 4, 1), pltpu.roll(second, 4, 1)), 0.0)
            for step in (8, 16, 32, 64):
                x = x + pltpu.roll(x, step, 1)
            return x

        count_w = spread(count_side, count_own)
        count_e = spread(count_own, count_side)

        for g in range(groups):
            kvec = (lane32 // 8 + g * GROUP).astype(F32)
            own_n, own_s = rows_in[N - 2, levels + g], rows_in[S - 2, levels + g]
            results = []
            for side in (W, E):
                if side == W:
                    counts = count_w
                    north = jnp.where(left8, corners_in[NW - 4, g], own_n)
                    south = jnp.where(left8, corners_in[SW - 4, g], own_s)
                    blocks = [jnp.where(left24, edges_in[W, f, g], edges[f, g]) for f in range(4)]
                else:
                    counts = count_e
                    north = jnp.where(left8, own_n, corners_in[NE - 4, g])
                    south = jnp.where(left8, own_s, corners_in[SE - 4, g])
                    blocks = [jnp.where(left24, edges[f, g], edges_in[E, f, g]) for f in range(4)]
                active = jnp.where(counts > kvec, 1.0, 0.0)
                results.append(tendencies(active, [with_rows(f, blocks[f], north, south) for f in range(4)]))
            for f in range(4):
                edge_out[f, g] = jnp.where(left24, results[1][f], results[0][f])

        rim = (lane24 < 2) | (lane24 >= 126)

        def blend(k, carry):
            g = k // GROUP
            back = (128 + 124 - 8 * (k % GROUP)) % 128
            for f in range(4):
                tend[f, k] = jnp.where(rim, pltpu.roll(edge_out[f, g], back, 1), tend[f, k])
            return carry

        lax.fori_loop(0, levels, blend, 0)
        out_copies = [pltpu.make_async_copy(tend.at[f], tend_hbm.at[f], out_sem.at[f]) for f in range(4)]
        for copy in out_copies:
            copy.start()

        for copy in copies_b:
            copy.wait_recv()
        level = total([mid[...]] + [gather_b[j] for j in range(nline - 1)])
        for step in (32, 16, 8, 4, 2, 1):
            level = dd_add(level, (pltpu.roll(level[0], 128 - step, 1), pltpu.roll(level[1], 128 - step, 1)))

        def scalar(a, row):
            return jnp.broadcast_to(a[row:row + 1, 0:1], (8, 128))

        mu = []
        for n in range(8):
            row = 4 * (n % 2) + 2 * (n // 2 % 2) + n // 4
            mu.append((scalar(level[0], row), scalar(level[1], row)))
        x_poly, r_poly = cg_coefficients(mu)
        for t in range(3):
            rows = slice(8 * t, 8 * t + 8)
            basis = [(v[0][rows], v[1][rows]) for v in own_vectors]

            def combined(poly):
                parts = [dd_mul(c, b) for c, b in zip(poly, basis)]
                while len(parts) > 1:
                    parts = [dd_add(parts[i], parts[i + 1]) if i + 1 < len(parts) else parts[i]
                             for i in range(0, len(parts), 2)]
                return parts[0]

            height = combined(x_poly)
            x_ref[rows] = (height[0] + height[1]) * (40.0 / 65536.0)
            rest = combined(r_poly)
            d = own_diag[rows]
            r_ref[rows] = (d * rest[0] + d * rest[1]) * (1.0 / 65536.0)

        for copy in surf_copies + other_copies + copies_a + copies_b:
            copy.wait_send()
        for copy in out_copies:
            copy.wait()

    scratch = [
        pltpu.VMEM((24, 128), F32), pltpu.VMEM((24, 128), jnp.int32), pltpu.VMEM((24, 128), jnp.int32),
        pltpu.VMEM((4, levels, 24, 128), F32), pltpu.VMEM((4, levels, 24, 128), F32),
        pltpu.VMEM((3, 2, 8, 128), F32), pltpu.VMEM((2, 3, 2, 8, 128), F32), pltpu.VMEM((6, 2, 8, 128), F32),
        pltpu.VMEM((4, groups, 24, 128), F32), pltpu.VMEM((2, 4, groups, 24, 128), F32),
        pltpu.VMEM((entries, 8, 128), F32), pltpu.VMEM((entries, 8, 128), F32),
        pltpu.VMEM((2, entries, 8, 128), F32), pltpu.VMEM((4, groups, 8, 128), F32),
        pltpu.VMEM((4, groups, 24, 128), F32),
        pltpu.VMEM((8, 128), F32), pltpu.VMEM((nplane - 1, 8, 128), F32),
        pltpu.VMEM((8, 128), F32), pltpu.VMEM((nline - 1, 8, 128), F32),
        pltpu.SemaphoreType.DMA((7,)), pltpu.SemaphoreType.DMA((4,)),
        pltpu.SemaphoreType.DMA((16,)), pltpu.SemaphoreType.DMA((16,)),
        pltpu.SemaphoreType.DMA((nplane - 1,)), pltpu.SemaphoreType.DMA((nplane - 1,)),
        pltpu.SemaphoreType.DMA((nline - 1,)), pltpu.SemaphoreType.DMA((nline - 1,)),
    ]
    return kernel, scratch


def solution(mesh):
    nlon, nlat = mesh.shape["lon"], mesh.shape["lat"]
    names = list(mesh.axis_names)

    def per_device(surface_forcing, sea_mask, level_count, state):
        kernel, scratch = make_kernel(nlon, nlat, state.shape[1], names)
        return pl.pallas_call(
            kernel,
            out_shape=(
                jax.ShapeDtypeStruct(surface_forcing.shape, F32),
                jax.ShapeDtypeStruct(surface_forcing.shape, F32),
                jax.ShapeDtypeStruct(state.shape, F32),
            ),
            in_specs=[pl.BlockSpec(memory_space=pl.ANY)] * 4,
            out_specs=(
                pl.BlockSpec(memory_space=pltpu.VMEM),
                pl.BlockSpec(memory_space=pltpu.VMEM),
                pl.BlockSpec(memory_space=pl.ANY),
            ),
            scratch_shapes=scratch,
            compiler_params=pltpu.CompilerParams(collective_id=0, has_side_effects=True),
            name="ocean",
        )(surface_forcing, sea_mask, level_count, state)

    flat, deep = P("lat", "lon"), P(None, None, "lat", "lon")
    return jax.shard_map(
        per_device, mesh=mesh, in_specs=(flat, flat, flat, deep), out_specs=(flat, flat, deep), check_vma=False
    )
```

time: 204 us -> 41 us (0.20)
  starting transfers between devices: 51.9 us -> 0 us
  other arithmetic: 51.2 us -> 0 us
  waiting for transfers between devices: 37.1 us -> 0 us
  Pallas kernels: 0 us -> 34.5 us
  local copies, waits for them, and re-layouts: 27.7 us -> 5.56 us
  blocking collectives: 20 us -> 0 us
  between operations: 14.1 us -> 0.64 us
    pallas_call x0 -> x1, Pallas kernels: none -> 34.5 us  [per_device(): pl.pallas_call(kernel, out_shape=(jax.ShapeDtypeStruct(surface_forcing.sh...]
    all_to_all x7 -> x0, starting transfers between devices: 32.4 us -> none  [copy_for_each(): return lax.all_to_all(copies, axis, split_axis=0, concat_axis=0, tiled=True)]
    all_to_all x7 -> x0, waiting for transfers between devices: 29.5 us -> none  [copy_for_each(): return lax.all_to_all(copies, axis, split_axis=0, concat_axis=0, tiled=True)]
    all_to_all x1 -> x0, blocking collectives: 20 us -> none  [copy_for_each(): return lax.all_to_all(copies, axis, split_axis=0, concat_axis=0, tiled=True)]
    ppermute x12 -> x0, starting transfers between devices: 19.5 us -> none  [the longest x6 11.8 us: with_halo(): lax.ppermute(head, axis, [((i + 1) % count, i) for i in range(count)])]
    mul x4 -> x0, other arithmetic: 17.4 us -> none  [the longest x1 12.5 us: tendency_of(): return trim_rims(active_wide, 2) * (-flux - viscosity * smoothed)]
    sub x4 -> x0, other arithmetic: 12.8 us -> none  [the longest x1 11.8 us: laplace(): return east_part - west_part + north_part - south_part]
    concatenate x7 -> x0, other arithmetic: 9.85 us -> none  [the longest x4 5.37 us: in_one(): jnp.concatenate([a.reshape(-1) for a in arrays])]
  transfers between devices with their start and end apart: 19 -> 0, of which waited for: 12 -> 0; matrix products, arithmetic and copies ran while one was open for 16% -> 0% of each run, Pallas kernels for 0% -> 0%
where the time goes in v1:
time: 41 us; the launch traced here: 40.7 us
  Pallas kernels  34.5 us (84%)
  local copies, waits for them, and re-layouts  5.56 us (14%)
  between operations  0.64 us (2%)
    pallas_call x1, Pallas kernels, per_device(): pl.pallas_call(kernel, out_shape=(jax.ShapeDtypeStruct(surface_forcing.sh...  34.5 us
    unnamed x3, local copies, waits for them, and re-layouts  5.56 us

profile of v1, /device:TPU:1, one launch (start us, length us, event | category | flops | bytes accessed | tf_op | source)
XLA Modules:
  0.0 40.7 jit_solution(12502446091979936960)
XLA Ops:
  0.6 34.5 %ocean.1 = (f32[24,128]{1,0:T(8,128)}, f32[24,128]{1,0:T(8,128)}, f32[4,40,24,128]{3,2,1,0:T(8,128)}) custom-call(f32[24,128]{1,0:T(8,128)} %forcing_hbm.1, s32[24,128]{1,0:T(8,128)} %sea_hbm.1, s32[24,128]{1,0:T(8,128)} %count_hbm.1, f32[4,40,24,128]{3,2,1,0:T(8,128)} %state_hbm.1), custom_call_target="tpu_custom_call" | custom-call | tf_op jit(solution)/shard_map/ocean/pallas_call | solution.py:483
  35.1 1.3 %copy.10 = f32[24,128]{1,0:T(8,128)} copy(f32[24,128]{1,0:T(8,128)} %get-tuple-element.6) | data formatting | bytes 24576
  36.4 1.3 %copy.11 = f32[24,128]{1,0:T(8,128)} copy(f32[24,128]{1,0:T(8,128)} %get-tuple-element.7) | data formatting | bytes 24576
  37.8 2.9 %copy.12 = f32[4,40,24,128]{3,2,1,0:T(8,128)} copy(f32[4,40,24,128]{3,2,1,0:T(8,128)} %get-tuple-element.8) | data formatting | bytes 3932160

commit v2 on v1

--- a/solution.py
+++ b/solution.py
@@ -3,6 +3,7 @@
 from jax import lax
 from jax.experimental import pallas as pl
 from jax.experimental.pallas import tpu as pltpu
+from jax.sharding import Mesh
 from jax.sharding import PartitionSpec as P
 
 MESH = pl.DeviceIdType.MESH
@@ -10,6 +11,7 @@
 CORES = 2
 GROUP = 16
 VISC = 0.02
+UNROLL = 2
 DIRS = ((1, 0), (-1, 0), (0, 1), (0, -1), (1, 1), (-1, -1), (1, -1), (-1, 1))
 OPP = (1, 0, 3, 2, 5, 4, 7, 6)
 E, W, N, S, NE, SW, SE, NW = range(8)
@@ -59,12 +61,11 @@
     return -a[0], -a[1]
 
 
-def dd_div(a, b):
+def dd_inverse(b):
     r = 1.0 / b[0]
-    q = a[0] * r
-    p, e = two_prod(q, b[0])
-    rest = ((a[0] - p) - e) + (a[1] - q * b[1])
-    return quick(q, rest * r)
+    p, e = two_prod(r, b[0])
+    rest = ((1.0 - p) - e) - r * b[1]
+    return quick(r, rest * r)
 
 
 def iota(shape, dim):
@@ -85,7 +86,8 @@
     p, q = [one], [one]
     x = []
     for k in range(4):
-        alpha = dd_div(s[k], t[k + 1])
+        inverse = dd_inverse(t[k + 1])
+        alpha = dd_mul(s[k], inverse)
         minus = dd_neg(alpha)
         x = [dd_add(x[i], dd_mul(alpha, q[i])) if i < len(x) else dd_mul(alpha, q[i]) for i in range(k + 1)]
         moved = [dd_mul(minus, c) for c in q]
@@ -93,7 +95,7 @@
         if k < 3:
             last = 6 - k
             s_next = {j: dd_add(s[j], dd_mul(minus, t[j + 1])) for j in range(k + 1, last + 1)}
-            beta = dd_mul(minus, dd_div(s_next[k + 1], s[k]))
+            beta = dd_mul(dd_neg(s_next[k + 1]), inverse)
             t = {j: dd_add(s_next[j], dd_mul(beta, t[j])) for j in range(k + 2, last + 1)}
             s = s_next
             q = [dd_add(p[i], dd_mul(beta, q[i])) if i <= k else p[i] for i in range(k + 2)]
@@ -125,25 +127,18 @@
     return out
 
 
-def make_kernel(nlon, nlat, levels, names):
-    nplane = nlon // CORES
+def make_kernel(nx, ny, nlat, levels):
+    nplane = nx * ny
     nline = CORES * nlat
+    half = levels // 2
     groups = -(-levels // GROUP)
     entries = levels + groups
-    order = [names.index("lon"), names.index("lat")]
-
-    def device(lon, lat):
-        pair = (lon, lat)
-        return (pair[order.index(0)], pair[order.index(1)])
-
-    def kernel(forcing_hbm, sea_hbm, count_hbm, state_hbm, x_ref, r_ref, tend_hbm,
-               forcing, sea, count, state, tend, surf, surf_ew, surf_ns, edges, edges_in, rows_up, rows_down,
+    def kernel(forcing_hbm, sea_hbm, count_hbm, state_hbm, x_ref, r_ref, tend,
+               forcing, sea, count, state, surf, surf_ew, surf_ns, edges, edges_in, rows_up, rows_down,
                rows_in, corners_in, edge_out, partial, gather_a, mid, gather_b,
-               in_sem, out_sem, send_sem, recv_sem, send_a, recv_a, send_b, recv_b):
-        lon = lax.axis_index("lon")
-        lat = lax.axis_index("lat")
-        plane, core = lon // CORES, lon % CORES
-        line = core * nlat + lat
+               in_sem, send_sem, recv_sem, send_a, recv_a, send_b, recv_b):
+        x, y = lax.axis_index("x"), lax.axis_index("y")
+        core, lat = lax.axis_index("core"), lax.axis_index("lat")
 
         small = [pltpu.make_async_copy(a, b, in_sem.at[i]) for i, (a, b) in
                  enumerate(((forcing_hbm, forcing), (sea_hbm, sea), (count_hbm, count)))]
@@ -151,14 +146,31 @@
         for copy in small + large:
             copy.start()
 
-        near = [device((lon + dx + nlon) % nlon, (lat + dy + nlat) % nlat) for dx, dy in DIRS]
-        plane_peer = [device(((plane + j) % nplane) * CORES + core, lat) for j in range(1, nplane)]
-        line_peer = []
-        for j in range(1, nline):
-            other = (line + j) % nline
-            line_peer.append(device(plane * CORES + other // nlat, other % nlat))
+        flip = 1 - core
+        y_east, y_west = y + core, y + ny - flip
+        place = {
+            1: (lax.rem(x + lax.div(y_east, ny), nx), lax.rem(y_east, ny), flip),
+            -1: (lax.rem(x + nx - 1 + lax.div(y_west, ny), nx), lax.rem(y_west, ny), flip),
+            0: (x, y, core),
+        }
+        row = {1: lax.rem(lat + 1, nlat), -1: lax.rem(lat + nlat - 1, nlat), 0: lat}
+        near = [(*place[dx], row[dy]) for dx, dy in DIRS]
+
+        def hops(step, size):
+            return min(step, size - step)
+
+        plane_steps = sorted(((i, j) for i in range(nx) for j in range(ny) if i or j),
+                             key=lambda p: -hops(p[0], nx) - hops(p[1], ny))
+        xs = [x] + [lax.rem(x + i, nx) for i in range(1, nx)]
+        ys = [y] + [lax.rem(y + j, ny) for j in range(1, ny)]
+        plane_peer = [(xs[i], ys[j], core, lat) for i, j in plane_steps]
+        line_steps = sorted(((c, j) for c in range(CORES) for j in range(nlat) if c or j),
+                            key=lambda p: -hops(p[1], nlat))
+        lats = [lat] + [lax.rem(lat + j, nlat) for j in range(1, nlat)]
+        line_peer = [(x, y, (core, flip)[c], lats[j]) for c, j in line_steps]
         barrier = pltpu.get_barrier_semaphore()
-        peers = near + plane_peer + line_peer
+        far = [p for pair in zip(plane_peer, line_peer) for p in pair]
+        peers = far + near[4:] + near[:4] if nplane == nline else plane_peer + line_peer + near
         for peer in peers:
             pl.semaphore_signal(barrier, inc=1, device_id=peer, device_id_type=MESH)
 
@@ -173,6 +185,8 @@
             surf[t, 0] = wet[rows].astype(F32)
             surf[t, 1] = (sea[rows].astype(F32) * forcing[rows]) * 65536.0
 
+        partial[...] = jnp.zeros_like(partial)
+        mid[...] = jnp.zeros_like(mid)
         for copy in large:
             copy.wait()
 
@@ -221,21 +235,27 @@
             return pltpu.make_async_remote_copy(source, surf_slot(OPP[d]), send_sem.at[d], recv_sem.at[OPP[d]],
                                                 device_id=near[d], device_id_type=MESH)
 
-        def rows_copy(d):
+        def rows_copy(d, part):
             source = rows_up if DIRS[d][1] > 0 else rows_down
             if d < 4:
                 target = rows_in.at[OPP[d] - 2]
+                span = pl.ds(0, half) if part == 0 else pl.ds(half, entries - half)
+                source, target = source.at[span], target.at[span]
             else:
                 source, target = source.at[pl.ds(levels, groups)], corners_in.at[OPP[d] - 4]
-            return pltpu.make_async_remote_copy(source, target, send_sem.at[8 + d], recv_sem.at[8 + OPP[d]],
+            sem = 8 + 8 * part
+            return pltpu.make_async_remote_copy(source, target, send_sem.at[sem + d], recv_sem.at[sem + OPP[d]],
                                                 device_id=near[d], device_id_type=MESH)
 
         def edge_copy(d):
             return pltpu.make_async_remote_copy(edges, edges_in.at[OPP[d]], send_sem.at[8 + d], recv_sem.at[8 + OPP[d]],
                                                 device_id=near[d], device_id_type=MESH)
 
-        surf_copies = [surf_copy(d) for d in range(8)]
-        other_copies = [edge_copy(d) if d < 2 else rows_copy(d) for d in range(8)]
+        surf_copies = [surf_copy(d) for d in (NE, NW, SE, SW, N, S, E, W)]
+        first_rows = [rows_copy(d, 0) for d in (N, S)]
+        last_rows = [rows_copy(d, 1) for d in (N, S)]
+        edge_copies = [edge_copy(d) for d in (E, W)] + [rows_copy(d, 0) for d in (NE, NW, SE, SW)]
+        other_copies = first_rows + edge_copies + last_rows
         for copy in surf_copies + other_copies:
             copy.start()
         for copy in surf_copies:
@@ -322,9 +342,15 @@
         level = [fold(sums[2 * i], sums[2 * i + 1], sub < 4, 4) for i in range(4)]
         level = [fold(level[2 * i], level[2 * i + 1], sub % 4 < 2, 2) for i in range(2)]
         level = fold(level[0], level[1], sub % 2 < 1, 1)
-        far = (pltpu.roll(level[0], 64, 1), pltpu.roll(level[1], 64, 1))
-        level = dd_add(level, far)
-        partial[...] = jnp.where(lane < 64, level[0], level[1])
+        parts = [x.T for x in level]
+        parts = [tuple(p[8 * i:8 * i + 8] for p in parts) for i in range(16)]
+        while len(parts) > 1:
+            parts = [dd_add(parts[i], parts[i + 1]) for i in range(0, len(parts), 2)]
+        level = parts[0]
+        for step in (4, 2, 1):
+            level = dd_add(tuple(p[:step] for p in level), tuple(p[step:2 * step] for p in level))
+        partial[0:1, 0:8] = level[0]
+        partial[1:2, 0:8] = level[1]
 
         copies_a = [pltpu.make_async_remote_copy(partial, gather_a.at[j], send_a.at[j], recv_a.at[j],
                                                  device_id=plane_peer[j], device_id_type=MESH)
@@ -332,18 +358,15 @@
         for copy in copies_a:
             copy.start()
 
-        def unpacked(message):
-            return message, pltpu.roll(message, 64, 1)
-
-        def total(messages):
-            parts = [unpacked(m) for m in messages]
+        def total(own, others, number):
+            parts = [(own[0:1], own[1:2])] + [(others[j, 0:1], others[j, 1:2]) for j in range(number)]
             while len(parts) > 1:
                 parts = [dd_add(parts[i], parts[i + 1]) if i + 1 < len(parts) else parts[i]
                          for i in range(0, len(parts), 2)]
             return parts[0]
 
-        for d in (N, S):
-            other_copies[d].wait_recv()
+        for copy in first_rows:
+            copy.wait_recv()
         count_own = jnp.concatenate([depth[0][:24], jnp.where(sub < 4, depth[0][24:32], depth[0][32:40])], 0)
         count_side = jnp.concatenate([depth[1][:24], jnp.where(sub < 4, depth[1][24:32], depth[1][32:40])], 0)
 
@@ -352,28 +375,38 @@
             down = pltpu.roll(south, 6 - 2 * f, 0) if f < 3 else south
             return jnp.concatenate([block, jnp.where(sub < 4, up, down)], 0)
 
-        def main(k, carry):
+        def main(k):
             active = jnp.where(count_own > k.astype(F32), 1.0, 0.0)
             north, south = rows_in[N - 2, k], rows_in[S - 2, k]
             quads = [with_rows(f, state[f, k], north, south) for f in range(4)]
             for f, value in enumerate(tendencies(active, quads)):
                 tend[f, k] = value
-            return carry
-
-        lax.fori_loop(0, levels, main, 0)
+
+        def unrolled(body, first, last, by):
+            def step(i, carry):
+                for j in range(by):
+                    body(first + i * by + j)
+                return carry
+            lax.fori_loop(0, (last - first) // by, step, 0)
+
+        unrolled(main, 0, half, UNROLL)
 
         for copy in copies_a:
             copy.wait_recv()
-        hi, lo = total([partial[...]] + [gather_a[j] for j in range(nplane - 1)])
-        mid[...] = jnp.where(lane < 64, hi, pltpu.roll(lo, 64, 1))
+        hi, lo = total(partial, gather_a, nplane - 1)
+        mid[0:1] = hi
+        mid[1:2] = lo
         copies_b = [pltpu.make_async_remote_copy(mid, gather_b.at[j], send_b.at[j], recv_b.at[j],
                                                  device_id=line_peer[j], device_id_type=MESH)
                     for j in range(nline - 1)]
         for copy in copies_b:
             copy.start()
 
-        for d in (E, W, NE, SW, SE, NW):
-            other_copies[d].wait_recv()
+        for copy in last_rows:
+            copy.wait_recv()
+        unrolled(main, half, levels, UNROLL)
+        for copy in edge_copies:
+            copy.wait_recv()
         lane32 = iota((32, 128), 1)
         left32, left24, left8 = lane32 % 8 < 4, lane24 % 8 < 4, lane % 8 < 4
 
@@ -408,31 +441,25 @@
 
         rim = (lane24 < 2) | (lane24 >= 126)
 
-        def blend(k, carry):
+        def blend(k):
             g = k // GROUP
             back = (128 + 124 - 8 * (k % GROUP)) % 128
             for f in range(4):
                 tend[f, k] = jnp.where(rim, pltpu.roll(edge_out[f, g], back, 1), tend[f, k])
-            return carry
-
-        lax.fori_loop(0, levels, blend, 0)
-        out_copies = [pltpu.make_async_copy(tend.at[f], tend_hbm.at[f], out_sem.at[f]) for f in range(4)]
-        for copy in out_copies:
-            copy.start()
+
+        unrolled(blend, 0, levels, 8)
 
         for copy in copies_b:
             copy.wait_recv()
-        level = total([mid[...]] + [gather_b[j] for j in range(nline - 1)])
-        for step in (32, 16, 8, 4, 2, 1):
-            level = dd_add(level, (pltpu.roll(level[0], 128 - step, 1), pltpu.roll(level[1], 128 - step, 1)))
-
-        def scalar(a, row):
-            return jnp.broadcast_to(a[row:row + 1, 0:1], (8, 128))
+        level = total(mid, gather_b, nline - 1)
+
+        def scalar(a, n):
+            return jnp.broadcast_to(a[0:1, n:n + 1], (8, 128))
 
         mu = []
         for n in range(8):
-            row = 4 * (n % 2) + 2 * (n // 2 % 2) + n // 4
-            mu.append((scalar(level[0], row), scalar(level[1], row)))
+            at = 4 * (n % 2) + 2 * (n // 2 % 2) + n // 4
+            mu.append((scalar(level[0], at), scalar(level[1], at)))
         x_poly, r_poly = cg_coefficients(mu)
         for t in range(3):
             rows = slice(8 * t, 8 * t + 8)
@@ -453,52 +480,71 @@
 
         for copy in surf_copies + other_copies + copies_a + copies_b:
             copy.wait_send()
-        for copy in out_copies:
-            copy.wait()
 
     scratch = [
         pltpu.VMEM((24, 128), F32), pltpu.VMEM((24, 128), jnp.int32), pltpu.VMEM((24, 128), jnp.int32),
-        pltpu.VMEM((4, levels, 24, 128), F32), pltpu.VMEM((4, levels, 24, 128), F32),
+        pltpu.VMEM((4, levels, 24, 128), F32),
         pltpu.VMEM((3, 2, 8, 128), F32), pltpu.VMEM((2, 3, 2, 8, 128), F32), pltpu.VMEM((6, 2, 8, 128), F32),
         pltpu.VMEM((4, groups, 24, 128), F32), pltpu.VMEM((2, 4, groups, 24, 128), F32),
         pltpu.VMEM((entries, 8, 128), F32), pltpu.VMEM((entries, 8, 128), F32),
         pltpu.VMEM((2, entries, 8, 128), F32), pltpu.VMEM((4, groups, 8, 128), F32),
         pltpu.VMEM((4, groups, 24, 128), F32),
-        pltpu.VMEM((8, 128), F32), pltpu.VMEM((nplane - 1, 8, 128), F32),
-        pltpu.VMEM((8, 128), F32), pltpu.VMEM((nline - 1, 8, 128), F32),
-        pltpu.SemaphoreType.DMA((7,)), pltpu.SemaphoreType.DMA((4,)),
-        pltpu.SemaphoreType.DMA((16,)), pltpu.SemaphoreType.DMA((16,)),
+        pltpu.VMEM((2, 128), F32), pltpu.VMEM((nplane - 1, 2, 128), F32),
+        pltpu.VMEM((2, 128), F32), pltpu.VMEM((nline - 1, 2, 128), F32),
+        pltpu.SemaphoreType.DMA((7,)),
+        pltpu.SemaphoreType.DMA((24,)), pltpu.SemaphoreType.DMA((24,)),
         pltpu.SemaphoreType.DMA((nplane - 1,)), pltpu.SemaphoreType.DMA((nplane - 1,)),
         pltpu.SemaphoreType.DMA((nline - 1,)), pltpu.SemaphoreType.DMA((nline - 1,)),
     ]
     return kernel, scratch
 
 
+def hand_out(x_ref, r_ref, tend_ref, x_out, r_out, tend_out, sem):
+    copies = [pltpu.make_async_copy(tend_ref.at[f], tend_out.at[f], sem.at[f]) for f in range(4)]
+    copies += [pltpu.make_async_copy(x_ref, x_out, sem.at[4]), pltpu.make_async_copy(r_ref, r_out, sem.at[5])]
+    for copy in copies:
+        copy.start()
+    for copy in copies:
+        copy.wait()
+
+
 def solution(mesh):
     nlon, nlat = mesh.shape["lon"], mesh.shape["lat"]
-    names = list(mesh.axis_names)
+    nplane = nlon // CORES
+    nx = max(n for n in range(1, nplane + 1) if nplane % n == 0 and n * n <= nplane)
+    ny = nplane // nx
+    finer = Mesh(mesh.devices.reshape(nx, ny, CORES, nlat), ("x", "y", "core", "lat"))
 
     def per_device(surface_forcing, sea_mask, level_count, state):
-        kernel, scratch = make_kernel(nlon, nlat, state.shape[1], names)
-        return pl.pallas_call(
+        kernel, scratch = make_kernel(nx, ny, nlat, state.shape[1])
+        results = pl.pallas_call(
             kernel,
             out_shape=(
-                jax.ShapeDtypeStruct(surface_forcing.shape, F32),
-                jax.ShapeDtypeStruct(surface_forcing.shape, F32),
-                jax.ShapeDtypeStruct(state.shape, F32),
+                pltpu.VMEM(surface_forcing.shape, F32),
+                pltpu.VMEM(surface_forcing.shape, F32),
+                pltpu.VMEM(state.shape, F32),
             ),
             in_specs=[pl.BlockSpec(memory_space=pl.ANY)] * 4,
             out_specs=(
                 pl.BlockSpec(memory_space=pltpu.VMEM),
                 pl.BlockSpec(memory_space=pltpu.VMEM),
-                pl.BlockSpec(memory_space=pl.ANY),
+                pl.BlockSpec(memory_space=pltpu.VMEM),
             ),
             scratch_shapes=scratch,
-            compiler_params=pltpu.CompilerParams(collective_id=0, has_side_effects=True),
+            compiler_params=pltpu.CompilerParams(collective_id=0, has_side_effects=True, vmem_limit_bytes=65_030_000),
             name="ocean",
         )(surface_forcing, sea_mask, level_count, state)
-
-    flat, deep = P("lat", "lon"), P(None, None, "lat", "lon")
+        return pl.pallas_call(
+            hand_out,
+            out_shape=tuple(jax.ShapeDtypeStruct(r.shape, F32) for r in results),
+            in_specs=[pl.BlockSpec(memory_space=pltpu.VMEM)] * 3,
+            out_specs=[pl.BlockSpec(memory_space=pl.ANY)] * 3,
+            scratch_shapes=[pltpu.SemaphoreType.DMA((6,))],
+            compiler_params=pltpu.CompilerParams(vmem_limit_bytes=8 * 2**20),
+            name="hand_out",
+        )(*results)
+
+    flat, deep = P("lat", ("x", "y", "core")), P(None, None, "lat", ("x", "y", "core"))
     return jax.shard_map(
-        per_device, mesh=mesh, in_specs=(flat, flat, flat, deep), out_specs=(flat, flat, deep), check_vma=False
+        per_device, mesh=finer, in_specs=(flat, flat, flat, deep), out_specs=(flat, flat, deep), check_vma=False
     )

time: 41 us -> 29.6 us (0.72)
  Pallas kernels: 34.5 us -> 28.8 us
  local copies, waits for them, and re-layouts: 5.56 us -> 0 us
    pallas_call x1 -> x2, Pallas kernels: 34.5 us -> 28.8 us  [the longest x1 27.4 us: per_device(): pl.pallas_call(kernel, out_shape=(pltpu.VMEM(surface_forcing.shape, F32),...]
    unnamed x3 -> x0, local copies, waits for them, and re-layouts: 5.56 us -> none
where the time goes in v2:
time: 29.6 us; the launch traced here: 29.4 us
  Pallas kernels  28.8 us (97%)
  between operations  0.64 us (2%)
    pallas_call x1, Pallas kernels, per_device(): pl.pallas_call(kernel, out_shape=(pltpu.VMEM(surface_forcing.shape, F32),...  27.4 us
    pallas_call x1, Pallas kernels, per_device(): pl.pallas_call(hand_out, out_shape=tuple((jax.ShapeDtypeStruct(r.shape, F...  1.32 us

profile of v2, /device:TPU:1, one launch (start us, length us, event | category | flops | bytes accessed | tf_op | source)
XLA Modules:
  0.0 29.4 jit_solution(14365115587111238578)
XLA Ops:
  0.6 27.4 %ocean.1 = (f32[24,128]{1,0:T(8,128)S(1)}, f32[24,128]{1,0:T(8,128)S(1)}, f32[4,40,24,128]{3,2,1,0:T(8,128)S(1)}) custom-call(f32[24,128]{1,0:T(8,128)} %forcing_hbm.1, s32[24,128]{1,0:T(8,128)} %sea_hbm.1, s32[24,128]{1,0:T(8,128)} %count_hbm.1, f32[4,40,24,128]{3,2,1,0:T(8,128)} %state_hbm.1), custom_call_target="tpu_custom_call" | custom-call | tf_op jit(solution)/shard_map/ocean/pallas_call | solution.py:520
  28.1 1.3 %hand_out.1 = (f32[24,128]{1,0:T(8,128)}, f32[24,128]{1,0:T(8,128)}, f32[4,40,24,128]{3,2,1,0:T(8,128)}) custom-call(f32[24,128]{1,0:T(8,128)S(1)} %get-tuple-element.6.x_ref, f32[24,128]{1,0:T(8,128)S(1)} %get-tuple-element.7.r_ref, f32[4,40,24,128]{3,2,1,0:T(8,128)S(1)} %get-tuple-element.8.tend_ref), custom_call_target="tpu_custom_call" | custom-call | tf_op jit(solution)/shard_map/hand_out/pallas_call | solution.py:537

commit v3 on v2

--- a/solution.py
+++ b/solution.py
@@ -12,6 +12,7 @@
 GROUP = 16
 VISC = 0.02
 UNROLL = 2
+FINISH = 8
 DIRS = ((1, 0), (-1, 0), (0, 1), (0, -1), (1, 1), (-1, -1), (1, -1), (-1, 1))
 OPP = (1, 0, 3, 2, 5, 4, 7, 6)
 E, W, N, S, NE, SW, SE, NW = range(8)
@@ -41,10 +42,10 @@
     return p, ((ah * bh - p) + ah * bl + al * bh) + al * bl
 
 
-def int_prod(w, h):
-    p = w * h
-    a, b = split(h)
-    return p, (w * a - p) + w * b
+def short(hi, lo):
+    t = 257.0 * hi
+    h = t - (t - hi)
+    return h, (hi - h) + lo
 
 
 def dd_add(a, b):
@@ -102,47 +103,60 @@
     return x, p
 
 
-def tendencies(active, quads):
-    east = shift_lanes(active, 1)
-    north = shift_rows(active, 1)
-    face_e = active * east
-    face_n = active * north
-    count = face_e + shift_lanes(face_e, -1) + face_n + shift_rows(face_n, -1)
-    u, v = quads[2], quads[3]
-    flow_e = (0.25 * face_e) * (u + shift_lanes(u, 1))
-    flow_n = (0.25 * face_n) * (v + shift_rows(v, 1))
+def first_pass(active, quads, masked, laps, weight):
     own = slice(0, 24)
-    flow_w = shift_lanes(flow_e, -1)[own]
-    flow_s = shift_rows(flow_n, -1)[own]
-    flow_e, flow_n = flow_e[own], flow_n[own]
+    face_e, face_w = active * shift_lanes(active, 1), active * shift_lanes(active, -1)
+    face_n, face_s = active * shift_rows(active, 1), active * shift_rows(active, -1)
+    count = (face_e + face_w) + (face_n + face_s)
+    weight[...] = VISC * active[own]
+    visc_count = VISC * count[own]
+    near = []
+    for f, q in enumerate(quads):
+        q = active * q
+        masked[f, 0:8] = q[24:32]
+        masked[f, 8:40] = q
+        masked[f, 40:48] = q[0:8]
+        near.append((q, shift_lanes(q, 1), shift_lanes(q, -1)))
+    u, ue, uw = (x[own] for x in near[2])
+    v = near[3][0][own]
+    flow_e = (0.25 * face_e[own]) * (u + ue)
+    flow_w = (0.25 * face_w[own]) * (u + uw)
+    flow_n = (0.25 * face_n[own]) * (v + masked[3, 9:33])
+    flow_s = (0.25 * face_s[own]) * (v + masked[3, 7:31])
     net = (flow_e - flow_w) + (flow_n - flow_s)
     out = []
-    for q in quads:
-        q = active * q
-        qe, qw, qn, qs = shift_lanes(q, 1), shift_lanes(q, -1), shift_rows(q, 1), shift_rows(q, -1)
+    for f, (q, qe, qw) in enumerate(near):
+        qn, qs = masked[f, 9:41], masked[f, 7:39]
         lap = active * ((qe + qw) + (qn + qs)) - count * q
-        around = (shift_lanes(lap, 1) + shift_lanes(lap, -1)) + (shift_rows(lap, 1) + shift_rows(lap, -1))
+        laps[f, 0:8] = lap[24:32]
+        laps[f, 8:40] = lap
         flux = (net * q[own] + flow_e * qe[own]) + (flow_n * qn[own] - flow_w * qw[own]) - flow_s * qs[own]
-        out.append(VISC * (count[own] * lap[own] - active[own] * around[own]) - flux)
+        out.append(visc_count * lap[own] - flux)
     return out
+
+
+def second_pass(f, laps, weight):
+    lap = laps[f, 8:32]
+    around = (shift_lanes(lap, 1) + shift_lanes(lap, -1)) + (laps[f, 9:33] + laps[f, 7:31])
+    return weight[...] * around
 
 
 def make_kernel(nx, ny, nlat, levels):
     nplane = nx * ny
     nline = CORES * nlat
-    half = levels // 2
+    half = 3 * levels // 5
     groups = -(-levels // GROUP)
     entries = levels + groups
     def kernel(forcing_hbm, sea_hbm, count_hbm, state_hbm, x_ref, r_ref, tend,
-               forcing, sea, count, state, surf, surf_ew, surf_ns, edges, edges_in, rows_up, rows_down,
-               rows_in, corners_in, edge_out, partial, gather_a, mid, gather_b,
-               in_sem, send_sem, recv_sem, send_a, recv_a, send_b, recv_b):
+               forcing, sea, count, state, surf, surf_in, edges, edges_in, rows_up, rows_down,
+               rows_a, rows_b, corners_in, counts, masked, laps, weight, edge_out, partial, gather_a, mid, gather_b, in_sem, send_sem, recv_sem, ready):
         x, y = lax.axis_index("x"), lax.axis_index("y")
         core, lat = lax.axis_index("core"), lax.axis_index("lat")
 
         small = [pltpu.make_async_copy(a, b, in_sem.at[i]) for i, (a, b) in
                  enumerate(((forcing_hbm, forcing), (sea_hbm, sea), (count_hbm, count)))]
-        large = [pltpu.make_async_copy(state_hbm.at[f], state.at[f], in_sem.at[3 + f]) for f in range(4)]
+        large = [pltpu.make_async_copy(state_hbm.at[pl.ds(2 * f, 2)], state.at[pl.ds(2 * f, 2)], in_sem.at[3 + f])
+                 for f in range(2)]
         for copy in small + large:
             copy.start()
 
@@ -169,8 +183,11 @@
         lats = [lat] + [lax.rem(lat + j, nlat) for j in range(1, nlat)]
         line_peer = [(x, y, (core, flip)[c], lats[j]) for c, j in line_steps]
         barrier = pltpu.get_barrier_semaphore()
-        far = [p for pair in zip(plane_peer, line_peer) for p in pair]
-        peers = far + near[4:] + near[:4] if nplane == nline else plane_peer + line_peer + near
+        column = [(x, p, core, lat) for p in ys[1:]]
+        rows = [(p, y, core, lat) for p in xs[1:]]
+        along = [(x, y, c, lax.rem(lat + j, nlat)) for j in (2, nlat - 2, 1, nlat - 1) for c in (core, flip)]
+        relay = column + [(x, y, core, lax.rem(lat + j, nlat)) for j in (2, nlat - 2)]
+        peers = near[4:] + along[:4] + column + rows + near[:4] + along[4:] + [(x, y, flip, lat)]
         for peer in peers:
             pl.semaphore_signal(barrier, inc=1, device_id=peer, device_id_type=MESH)
 
@@ -187,6 +204,40 @@
 
         partial[...] = jnp.zeros_like(partial)
         mid[...] = jnp.zeros_like(mid)
+        pl.semaphore_wait(barrier, len(peers))
+
+        def remote(source, target, i, peer):
+            return pltpu.make_async_remote_copy(source, target, send_sem.at[i], recv_sem.at[i],
+                                                device_id=peer, device_id_type=MESH)
+
+        def surf_slot(d):
+            return surf_in.at[pl.ds(3 * d, 3)] if d < 2 else surf_in.at[pl.ds(4 + d, 1)]
+
+        def surf_copy(d):
+            source = surf if d < 2 else surf.at[pl.ds(2 if DIRS[d][1] > 0 else 0, 1)]
+            return remote(source, surf_slot(OPP[d]), 0, near[d])
+
+        def rows_copy(d, part):
+            source = rows_up if DIRS[d][1] > 0 else rows_down
+            span = pl.ds(0, half) if part == 0 else pl.ds(half, entries - half)
+            return remote(source.at[span], (rows_a, rows_b)[part].at[OPP[d] - 2], 1 + part, near[d])
+
+        def corner_copy(d):
+            source = rows_up if DIRS[d][1] > 0 else rows_down
+            return remote(source.at[pl.ds(levels, groups)], corners_in.at[OPP[d] - 4], 3, near[d])
+
+        def edge_copy(d):
+            return remote(edges, edges_in.at[OPP[d]], 4, near[d])
+
+        landing = (surf_in, rows_a, rows_b, corners_in, edges_in, gather_a, gather_b)
+
+        def wait_all(sem, i):
+            pltpu.make_async_copy(landing[i], landing[i], sem.at[i]).wait()
+
+        for d in (NE, NW, SE, SW, N, S, E, W):
+            surf_copy(d).start()
+        for peer in relay:
+            pl.semaphore_signal(ready, inc=1, device_id=peer, device_id_type=MESH)
         for copy in large:
             copy.wait()
 
@@ -201,7 +252,6 @@
                 edges[f, g] = packed
             return carry
 
-        lax.fori_loop(0, 4, pack_edges, 0)
 
         def packed_rows(tile_of):
             up, down = None, None
@@ -220,55 +270,30 @@
             return carry
 
         lax.fori_loop(0, levels, pack_rows, 0)
+        for d in (N, S):
+            rows_copy(d, 0).start()
+        lax.fori_loop(0, 4, pack_edges, 0)
         for g in range(groups):
             up, down = packed_rows(lambda f, rows: edges[f, g, rows])
             rows_up[levels + g] = up
             rows_down[levels + g] = down
 
-        pl.semaphore_wait(barrier, len(peers))
-
-        def surf_slot(d):
-            return surf_ew.at[d] if d < 2 else surf_ns.at[d - 2]
-
-        def surf_copy(d):
-            source = surf if d < 2 else surf.at[2 if DIRS[d][1] > 0 else 0]
-            return pltpu.make_async_remote_copy(source, surf_slot(OPP[d]), send_sem.at[d], recv_sem.at[OPP[d]],
-                                                device_id=near[d], device_id_type=MESH)
-
-        def rows_copy(d, part):
-            source = rows_up if DIRS[d][1] > 0 else rows_down
-            if d < 4:
-                target = rows_in.at[OPP[d] - 2]
-                span = pl.ds(0, half) if part == 0 else pl.ds(half, entries - half)
-                source, target = source.at[span], target.at[span]
-            else:
-                source, target = source.at[pl.ds(levels, groups)], corners_in.at[OPP[d] - 4]
-            sem = 8 + 8 * part
-            return pltpu.make_async_remote_copy(source, target, send_sem.at[sem + d], recv_sem.at[sem + OPP[d]],
-                                                device_id=near[d], device_id_type=MESH)
-
-        def edge_copy(d):
-            return pltpu.make_async_remote_copy(edges, edges_in.at[OPP[d]], send_sem.at[8 + d], recv_sem.at[8 + OPP[d]],
-                                                device_id=near[d], device_id_type=MESH)
-
-        surf_copies = [surf_copy(d) for d in (NE, NW, SE, SW, N, S, E, W)]
-        first_rows = [rows_copy(d, 0) for d in (N, S)]
-        last_rows = [rows_copy(d, 1) for d in (N, S)]
-        edge_copies = [edge_copy(d) for d in (E, W)] + [rows_copy(d, 0) for d in (NE, NW, SE, SW)]
-        other_copies = first_rows + edge_copies + last_rows
-        for copy in surf_copies + other_copies:
-            copy.start()
-        for copy in surf_copies:
-            copy.wait_recv()
+        for d in (E, W):
+            edge_copy(d).start()
+        for d in (NE, NW, SE, SW):
+            corner_copy(d).start()
+        for d in (N, S):
+            rows_copy(d, 1).start()
+        wait_all(recv_sem, 0)
 
         has_north = jnp.where(lat < nlat - 1, 1.0, 0.0).astype(F32)
         has_south = jnp.where(lat > 0, 1.0, 0.0).astype(F32)
 
         def wide(v):
-            own = [surf[t, v] for t in range(3)] + [surf_ns[N - 2, v] * has_north, surf_ns[S - 2, v] * has_south]
-            side = [jnp.where(lane < 64, surf_ew[E, t, v], surf_ew[W, t, v]) for t in range(3)]
-            side.append(jnp.where(lane < 64, surf_ns[NE - 2, v], surf_ns[NW - 2, v]) * has_north)
-            side.append(jnp.where(lane < 64, surf_ns[SE - 2, v], surf_ns[SW - 2, v]) * has_south)
+            own = [surf[t, v] for t in range(3)] + [surf_in[4 + N, v] * has_north, surf_in[4 + S, v] * has_south]
+            side = [jnp.where(lane < 64, surf_in[t, v], surf_in[3 + t, v]) for t in range(3)]
+            side.append(jnp.where(lane < 64, surf_in[4 + NE, v], surf_in[4 + NW, v]) * has_north)
+            side.append(jnp.where(lane < 64, surf_in[4 + SE, v], surf_in[4 + SW, v]) * has_south)
             return jnp.concatenate(own, 0), jnp.concatenate(side, 0)
 
         lane40 = iota((40, 128), 1)
@@ -296,12 +321,10 @@
         inverse = [1.0 / diag[t] for t in range(2)]
 
         def over_diag(hi, lo, t):
-            q = hi * inverse[t]
-            a, b = split(q)
-            rest = ((hi - diag[t] * a) - diag[t] * b) + lo
-            return q, rest * inverse[t]
-
-        vectors = [[quick(*over_diag(force[t], jnp.zeros_like(force[t]), t)) for t in range(2)]]
+            q, rest = short(hi * inverse[t], 0.0)
+            return q, ((hi - diag[t] * q) + lo) * inverse[t]
+
+        vectors = [[short(*over_diag(force[t], 0.0, t)) for t in range(2)]]
         for k in range(4):
             last = vectors[-1]
             high = [move((last[0][0], last[1][0])) for move in moves]
@@ -310,24 +333,23 @@
             for t in range(2):
                 if k == 3 and t == 1:
                     continue
-                terms = [int_prod(faces[t][i], high[i][t]) for i in range(4)]
-                fine = [faces[t][i] * low[i][t] + terms[i][1] for i in range(4)]
-                s0, e0 = two_sum(terms[0][0], terms[1][0])
-                s1, e1 = two_sum(terms[2][0], terms[3][0])
+                terms = [faces[t][i] * high[i][t] for i in range(4)]
+                fine = [faces[t][i] * low[i][t] for i in range(4)]
+                s0, e0 = two_sum(terms[0], terms[1])
+                s1, e1 = two_sum(terms[2], terms[3])
                 s, e2 = two_sum(s0, s1)
                 rest = ((e0 + e1) + e2) + ((fine[0] + fine[1]) + (fine[2] + fine[3]))
                 q, q_low = over_diag(s, rest, t)
                 s, e = two_sum(last[t][0], -q)
-                following.append(quick(s, e + (last[t][1] - q_low)))
+                following.append(short(s, e + (last[t][1] - q_low)))
             vectors.append(following)
-        own_vectors = [(v[0][0][:24], v[0][1][:24]) for v in vectors]
+        own_vectors = [quick(v[0][0][:24], v[0][1][:24]) for v in vectors]
         own_diag = diag[0][:24]
+        weighted = [quick(own_diag * v[0][0][:24], own_diag * v[0][1][:24]) for v in vectors[:4]]
 
         sums = []
         for n in range(8):
-            a, b = own_vectors[n // 2], own_vectors[n - n // 2]
-            p, e = int_prod(own_diag, a[0])
-            product = dd_mul(quick(p, e + own_diag * a[1]), b)
+            product = dd_mul(weighted[n // 2], own_vectors[n - n // 2])
             tiles = [(product[0][8 * i:8 * i + 8], product[1][8 * i:8 * i + 8]) for i in range(3)]
             sums.append(dd_add(dd_add(tiles[0], tiles[1]), tiles[2]))
 
@@ -352,11 +374,9 @@
         partial[0:1, 0:8] = level[0]
         partial[1:2, 0:8] = level[1]
 
-        copies_a = [pltpu.make_async_remote_copy(partial, gather_a.at[j], send_a.at[j], recv_a.at[j],
-                                                 device_id=plane_peer[j], device_id_type=MESH)
-                    for j in range(nplane - 1)]
-        for copy in copies_a:
-            copy.start()
+        pl.semaphore_wait(ready, len(relay))
+        for j, peer in enumerate(plane_peer):
+            remote(partial, gather_a.at[j], 5, peer).start()
 
         def total(own, others, number):
             parts = [(own[0:1], own[1:2])] + [(others[j, 0:1], others[j, 1:2]) for j in range(number)]
@@ -365,8 +385,7 @@
                          for i in range(0, len(parts), 2)]
             return parts[0]
 
-        for copy in first_rows:
-            copy.wait_recv()
+        wait_all(recv_sem, 1)
         count_own = jnp.concatenate([depth[0][:24], jnp.where(sub < 4, depth[0][24:32], depth[0][32:40])], 0)
         count_side = jnp.concatenate([depth[1][:24], jnp.where(sub < 4, depth[1][24:32], depth[1][32:40])], 0)
 
@@ -375,40 +394,28 @@
             down = pltpu.roll(south, 6 - 2 * f, 0) if f < 3 else south
             return jnp.concatenate([block, jnp.where(sub < 4, up, down)], 0)
 
-        def main(k):
+        def main(k, slot, rows_in, base):
             active = jnp.where(count_own > k.astype(F32), 1.0, 0.0)
-            north, south = rows_in[N - 2, k], rows_in[S - 2, k]
+            north, south = rows_in[N - 2, k - base], rows_in[S - 2, k - base]
             quads = [with_rows(f, state[f, k], north, south) for f in range(4)]
-            for f, value in enumerate(tendencies(active, quads)):
+            for f, value in enumerate(first_pass(active, quads, masked.at[slot], laps.at[k - base], weight.at[k - base])):
                 tend[f, k] = value
+
+        def finish(k, base):
+            for f in range(4):
+                tend[f, k] = tend[f, k] - second_pass(f, laps.at[k - base], weight.at[k - base])
 
         def unrolled(body, first, last, by):
             def step(i, carry):
                 for j in range(by):
-                    body(first + i * by + j)
+                    body(first + i * by + j, j)
                 return carry
             lax.fori_loop(0, (last - first) // by, step, 0)
 
-        unrolled(main, 0, half, UNROLL)
-
-        for copy in copies_a:
-            copy.wait_recv()
-        hi, lo = total(partial, gather_a, nplane - 1)
-        mid[0:1] = hi
-        mid[1:2] = lo
-        copies_b = [pltpu.make_async_remote_copy(mid, gather_b.at[j], send_b.at[j], recv_b.at[j],
-                                                 device_id=line_peer[j], device_id_type=MESH)
-                    for j in range(nline - 1)]
-        for copy in copies_b:
-            copy.start()
-
-        for copy in last_rows:
-            copy.wait_recv()
-        unrolled(main, half, levels, UNROLL)
-        for copy in edge_copies:
-            copy.wait_recv()
+        unrolled(lambda k, slot: main(k, slot, rows_a, 0), 0, half, UNROLL)
+        unrolled(lambda k, slot: finish(k, 0), 0, half, FINISH)
+
         lane32 = iota((32, 128), 1)
-        left32, left24, left8 = lane32 % 8 < 4, lane24 % 8 < 4, lane % 8 < 4
 
         def spread(first, second):
             x = jnp.where(lane32 < 8, jnp.where(lane32 < 4, pltpu.roll(first, 4, 1), pltpu.roll(second, 4, 1)), 0.0)
@@ -416,41 +423,60 @@
                 x = x + pltpu.roll(x, step, 1)
             return x
 
-        count_w = spread(count_side, count_own)
-        count_e = spread(count_own, count_side)
-
-        for g in range(groups):
-            kvec = (lane32 // 8 + g * GROUP).astype(F32)
-            own_n, own_s = rows_in[N - 2, levels + g], rows_in[S - 2, levels + g]
-            results = []
-            for side in (W, E):
-                if side == W:
-                    counts = count_w
-                    north = jnp.where(left8, corners_in[NW - 4, g], own_n)
-                    south = jnp.where(left8, corners_in[SW - 4, g], own_s)
-                    blocks = [jnp.where(left24, edges_in[W, f, g], edges[f, g]) for f in range(4)]
-                else:
-                    counts = count_e
-                    north = jnp.where(left8, own_n, corners_in[NE - 4, g])
-                    south = jnp.where(left8, own_s, corners_in[SE - 4, g])
-                    blocks = [jnp.where(left24, edges[f, g], edges_in[E, f, g]) for f in range(4)]
-                active = jnp.where(counts > kvec, 1.0, 0.0)
-                results.append(tendencies(active, [with_rows(f, blocks[f], north, south) for f in range(4)]))
+        counts[0] = spread(count_side, count_own)
+        counts[1] = spread(count_own, count_side)
+
+        wait_all(recv_sem, 5)
+        hi, lo = total(partial, gather_a, nplane - 1)
+        mid[0:1] = hi
+        mid[1:2] = lo
+        for j, peer in enumerate(line_peer):
+            remote(mid, gather_b.at[j], 6, peer).start()
+
+        wait_all(recv_sem, 2)
+        unrolled(lambda k, slot: main(k, slot, rows_b, half), half, levels, UNROLL)
+        unrolled(lambda k, slot: finish(k, half), half, levels, FINISH)
+        wait_all(recv_sem, 3)
+        wait_all(recv_sem, 4)
+        left24, left8 = lane24 % 8 < 4, lane % 8 < 4
+
+        def edge_active(side, g):
+            return jnp.where(counts[side] > (lane32 // 8 + g * GROUP).astype(F32), 1.0, 0.0)
+
+        def edge_first(g, side, slot):
+            if side == 0:
+                north = jnp.where(left8, corners_in[NW - 4, g], rows_b[N - 2, levels - half + g])
+                south = jnp.where(left8, corners_in[SW - 4, g], rows_b[S - 2, levels - half + g])
+                blocks = [jnp.where(left24, edges_in[W, f, g], edges[f, g]) for f in range(4)]
+            else:
+                north = jnp.where(left8, rows_b[N - 2, levels - half + g], corners_in[NE - 4, g])
+                south = jnp.where(left8, rows_b[S - 2, levels - half + g], corners_in[SE - 4, g])
+                blocks = [jnp.where(left24, edges[f, g], edges_in[E, f, g]) for f in range(4)]
+            quads = [with_rows(f, blocks[f], north, south) for f in range(4)]
+            at = 2 * g + side
+            return first_pass(edge_active(side, g), quads, masked.at[slot], laps.at[at], weight.at[at])
+
+        def edge(g):
+            west, east = edge_first(g, 0, 0), edge_first(g, 1, 1)
             for f in range(4):
-                edge_out[f, g] = jnp.where(left24, results[1][f], results[0][f])
+                edge_out[f, g] = jnp.where(left24, east[f], west[f])
+
+        def edge_finish(g):
+            for f in range(4):
+                west, east = (second_pass(f, laps.at[2 * g + i], weight.at[2 * g + i]) for i in range(2))
+                edge_out[f, g] = edge_out[f, g] - jnp.where(left24, east, west)
+
+        unrolled(lambda g, slot: edge(g), 0, groups, 1)
+        unrolled(lambda g, slot: edge_finish(g), 0, groups, groups)
 
         rim = (lane24 < 2) | (lane24 >= 126)
 
-        def blend(k):
-            g = k // GROUP
-            back = (128 + 124 - 8 * (k % GROUP)) % 128
+        for k in range(levels):
+            g, back = k // GROUP, (252 - 8 * (k % GROUP)) % 128
             for f in range(4):
                 tend[f, k] = jnp.where(rim, pltpu.roll(edge_out[f, g], back, 1), tend[f, k])
 
-        unrolled(blend, 0, levels, 8)
-
-        for copy in copies_b:
-            copy.wait_recv()
+        wait_all(recv_sem, 6)
         level = total(mid, gather_b, nline - 1)
 
         def scalar(a, n):
@@ -478,23 +504,24 @@
             d = own_diag[rows]
             r_ref[rows] = (d * rest[0] + d * rest[1]) * (1.0 / 65536.0)
 
-        for copy in surf_copies + other_copies + copies_a + copies_b:
-            copy.wait_send()
+        for i in range(7):
+            wait_all(send_sem, i)
 
     scratch = [
         pltpu.VMEM((24, 128), F32), pltpu.VMEM((24, 128), jnp.int32), pltpu.VMEM((24, 128), jnp.int32),
         pltpu.VMEM((4, levels, 24, 128), F32),
-        pltpu.VMEM((3, 2, 8, 128), F32), pltpu.VMEM((2, 3, 2, 8, 128), F32), pltpu.VMEM((6, 2, 8, 128), F32),
+        pltpu.VMEM((3, 2, 8, 128), F32), pltpu.VMEM((12, 2, 8, 128), F32),
         pltpu.VMEM((4, groups, 24, 128), F32), pltpu.VMEM((2, 4, groups, 24, 128), F32),
         pltpu.VMEM((entries, 8, 128), F32), pltpu.VMEM((entries, 8, 128), F32),
-        pltpu.VMEM((2, entries, 8, 128), F32), pltpu.VMEM((4, groups, 8, 128), F32),
+        pltpu.VMEM((2, half, 8, 128), F32), pltpu.VMEM((2, entries - half, 8, 128), F32),
+        pltpu.VMEM((4, groups, 8, 128), F32),
+        pltpu.VMEM((2, 32, 128), F32), pltpu.VMEM((UNROLL, 4, 48, 128), F32),
+        pltpu.VMEM((half, 4, 40, 128), F32), pltpu.VMEM((half, 24, 128), F32),
         pltpu.VMEM((4, groups, 24, 128), F32),
         pltpu.VMEM((2, 128), F32), pltpu.VMEM((nplane - 1, 2, 128), F32),
         pltpu.VMEM((2, 128), F32), pltpu.VMEM((nline - 1, 2, 128), F32),
-        pltpu.SemaphoreType.DMA((7,)),
-        pltpu.SemaphoreType.DMA((24,)), pltpu.SemaphoreType.DMA((24,)),
-        pltpu.SemaphoreType.DMA((nplane - 1,)), pltpu.SemaphoreType.DMA((nplane - 1,)),
-        pltpu.SemaphoreType.DMA((nline - 1,)), pltpu.SemaphoreType.DMA((nline - 1,)),
+        pltpu.SemaphoreType.DMA((5,)), pltpu.SemaphoreType.DMA((7,)), pltpu.SemaphoreType.DMA((7,)),
+        pltpu.SemaphoreType.REGULAR,
     ]
     return kernel, scratch
 

time: 29.6 us -> 27.1 us (0.916)
  Pallas kernels: 28.8 us -> 26.3 us
    pallas_call x1, Pallas kernels: 27.4 us -> 25 us  [per_device(): pl.pallas_call(kernel, out_shape=(pltpu.VMEM(surface_forcing.shape, F32),...]
where the time goes in v3:
time: 27.1 us; the launch traced here: 27 us
  Pallas kernels  26.3 us (97%)
  between operations  0.64 us (2%)
    pallas_call x1, Pallas kernels, per_device(): pl.pallas_call(kernel, out_shape=(pltpu.VMEM(surface_forcing.shape, F32),...  25 us
    pallas_call x1, Pallas kernels, per_device(): pl.pallas_call(hand_out, out_shape=tuple((jax.ShapeDtypeStruct(r.shape, F...  1.32 us

profile of v3, /device:TPU:1, one launch (start us, length us, event | category | flops | bytes accessed | tf_op | source)
XLA Modules:
  0.0 27.0 jit_solution(13022790673415547467)
XLA Ops:
  0.6 25.0 %ocean.1 = (f32[24,128]{1,0:T(8,128)S(1)}, f32[24,128]{1,0:T(8,128)S(1)}, f32[4,40,24,128]{3,2,1,0:T(8,128)S(1)}) custom-call(f32[24,128]{1,0:T(8,128)} %forcing_hbm.1, s32[24,128]{1,0:T(8,128)} %sea_hbm.1, s32[24,128]{1,0:T(8,128)} %count_hbm.1, f32[4,40,24,128]{3,2,1,0:T(8,128)} %state_hbm.1), custom_call_target="tpu_custom_call" | custom-call | tf_op jit(solution)/shard_map/ocean/pallas_call | solution.py:547
  25.7 1.3 %hand_out.1 = (f32[24,128]{1,0:T(8,128)}, f32[24,128]{1,0:T(8,128)}, f32[4,40,24,128]{3,2,1,0:T(8,128)}) custom-call(f32[24,128]{1,0:T(8,128)S(1)} %get-tuple-element.6.x_ref, f32[24,128]{1,0:T(8,128)S(1)} %get-tuple-element.7.r_ref, f32[4,40,24,128]{3,2,1,0:T(8,128)S(1)} %get-tuple-element.8.tend_ref), custom_call_target="tpu_custom_call" | custom-call | tf_op jit(solution)/shard_map/hand_out/pallas_call | solution.py:564

commit v4 on v3

--- a/solution.py
+++ b/solution.py
@@ -11,6 +11,7 @@
 CORES = 2
 GROUP = 16
 VISC = 0.02
+HALO = 5
 UNROLL = 2
 FINISH = 8
 DIRS = ((1, 0), (-1, 0), (0, 1), (0, -1), (1, 1), (-1, -1), (1, -1), (-1, 1))
@@ -148,7 +149,7 @@
     groups = -(-levels // GROUP)
     entries = levels + groups
     def kernel(forcing_hbm, sea_hbm, count_hbm, state_hbm, x_ref, r_ref, tend,
-               forcing, sea, count, state, surf, surf_in, edges, edges_in, rows_up, rows_down,
+               forcing, sea, count, state, surf, surf_in, surf_s, surf_b, edges, edges_in, rows_up, rows_down,
                rows_a, rows_b, corners_in, counts, masked, laps, weight, edge_out, partial, gather_a, mid, gather_b, in_sem, send_sem, recv_sem, ready):
         x, y = lax.axis_index("x"), lax.axis_index("y")
         core, lat = lax.axis_index("core"), lax.axis_index("lat")
@@ -187,7 +188,7 @@
         rows = [(p, y, core, lat) for p in xs[1:]]
         along = [(x, y, c, lax.rem(lat + j, nlat)) for j in (2, nlat - 2, 1, nlat - 1) for c in (core, flip)]
         relay = column + [(x, y, core, lax.rem(lat + j, nlat)) for j in (2, nlat - 2)]
-        peers = near[4:] + along[:4] + column + rows + near[:4] + along[4:] + [(x, y, flip, lat)]
+        peers = [near[NW], near[W]] + along[:4] + column + rows + along[4:] + [near[N], (x, y, flip, lat)]
         for peer in peers:
             pl.semaphore_signal(barrier, inc=1, device_id=peer, device_id_type=MESH)
 
@@ -210,12 +211,8 @@
             return pltpu.make_async_remote_copy(source, target, send_sem.at[i], recv_sem.at[i],
                                                 device_id=peer, device_id_type=MESH)
 
-        def surf_slot(d):
-            return surf_in.at[pl.ds(3 * d, 3)] if d < 2 else surf_in.at[pl.ds(4 + d, 1)]
-
-        def surf_copy(d):
-            source = surf if d < 2 else surf.at[pl.ds(2 if DIRS[d][1] > 0 else 0, 1)]
-            return remote(source, surf_slot(OPP[d]), 0, near[d])
+        def surf_copy(d, tiles, target, group):
+            return remote(surf.at[pl.ds(*tiles)], target, group, near[d])
 
         def rows_copy(d, part):
             source = rows_up if DIRS[d][1] > 0 else rows_down
@@ -229,13 +226,15 @@
         def edge_copy(d):
             return remote(edges, edges_in.at[OPP[d]], 4, near[d])
 
-        landing = (surf_in, rows_a, rows_b, corners_in, edges_in, gather_a, gather_b)
+        landing = (surf_in, rows_a, rows_b, corners_in, edges_in, gather_a, gather_b, surf_s, surf_b)
 
         def wait_all(sem, i):
             pltpu.make_async_copy(landing[i], landing[i], sem.at[i]).wait()
 
-        for d in (NE, NW, SE, SW, N, S, E, W):
-            surf_copy(d).start()
+        surf_copy(SE, (0, 2), surf_in.at[pl.ds(5, 2)], 0).start()
+        surf_copy(E, (0, 3), surf_in.at[pl.ds(0, 3)], 0).start()
+        surf_copy(S, (0, 2), surf_in.at[pl.ds(3, 2)], 0).start()
+        surf_copy(N, (2, 1), surf_s, 7).start()
         for peer in relay:
             pl.semaphore_signal(ready, inc=1, device_id=peer, device_id_type=MESH)
         for copy in large:
@@ -278,10 +277,6 @@
             rows_up[levels + g] = up
             rows_down[levels + g] = down
 
-        for d in (E, W):
-            edge_copy(d).start()
-        for d in (NE, NW, SE, SW):
-            corner_copy(d).start()
         for d in (N, S):
             rows_copy(d, 1).start()
         wait_all(recv_sem, 0)
@@ -289,11 +284,16 @@
         has_north = jnp.where(lat < nlat - 1, 1.0, 0.0).astype(F32)
         has_south = jnp.where(lat > 0, 1.0, 0.0).astype(F32)
 
-        def wide(v):
-            own = [surf[t, v] for t in range(3)] + [surf_in[4 + N, v] * has_north, surf_in[4 + S, v] * has_south]
-            side = [jnp.where(lane < 64, surf_in[t, v], surf_in[3 + t, v]) for t in range(3)]
-            side.append(jnp.where(lane < 64, surf_in[4 + NE, v], surf_in[4 + NW, v]) * has_north)
-            side.append(jnp.where(lane < 64, surf_in[4 + SE, v], surf_in[4 + SW, v]) * has_south)
+        def ahead(v):
+            own = [surf[t, v] for t in range(3)] + [surf_in[3 + t, v] for t in range(2)]
+            west = [surf_in[t, v] for t in range(3)] + [surf_in[5 + t, v] for t in range(2)]
+            return jnp.concatenate(own, 0), jnp.concatenate(west, 0)
+
+        def around_own(v):
+            own = [surf[t, v] for t in range(3)] + [surf_in[3, v] * has_north, surf_s[0, v] * has_south]
+            side = [jnp.where(lane < 64, surf_b[t, v], surf_in[t, v]) for t in range(3)]
+            side.append(jnp.where(lane < 64, surf_b[3, v], surf_in[5, v]) * has_north)
+            side.append(jnp.where(lane < 64, surf_b[4, v], surf_b[5, v]) * has_south)
             return jnp.concatenate(own, 0), jnp.concatenate(side, 0)
 
         lane40 = iota((40, 128), 1)
@@ -313,43 +313,53 @@
             return shift_rows(pair[0], -1), shift_rows(pair[1], -1)
 
         moves = (to_east, to_west, to_north, to_south)
-        depth = wide(0)
-        force = wide(1)
-        moved = [move(depth) for move in moves]
-        faces = [[jnp.minimum(depth[t], m[t]) for m in moved] for t in range(2)]
-        diag = [2.0 + ((faces[t][0] + faces[t][1]) + (faces[t][2] + faces[t][3])) for t in range(2)]
-        inverse = [1.0 / diag[t] for t in range(2)]
-
-        def over_diag(hi, lo, t):
-            q, rest = short(hi * inverse[t], 0.0)
-            return q, ((hi - diag[t] * q) + lo) * inverse[t]
-
-        vectors = [[short(*over_diag(force[t], 0.0, t)) for t in range(2)]]
-        for k in range(4):
-            last = vectors[-1]
-            high = [move((last[0][0], last[1][0])) for move in moves]
-            low = [move((last[0][1], last[1][1])) for move in moves]
-            following = []
-            for t in range(2):
-                if k == 3 and t == 1:
-                    continue
-                terms = [faces[t][i] * high[i][t] for i in range(4)]
-                fine = [faces[t][i] * low[i][t] for i in range(4)]
-                s0, e0 = two_sum(terms[0], terms[1])
-                s1, e1 = two_sum(terms[2], terms[3])
-                s, e2 = two_sum(s0, s1)
-                rest = ((e0 + e1) + e2) + ((fine[0] + fine[1]) + (fine[2] + fine[3]))
-                q, q_low = over_diag(s, rest, t)
-                s, e = two_sum(last[t][0], -q)
-                following.append(short(s, e + (last[t][1] - q_low)))
-            vectors.append(following)
-        own_vectors = [quick(v[0][0][:24], v[0][1][:24]) for v in vectors]
-        own_diag = diag[0][:24]
-        weighted = [quick(own_diag * v[0][0][:24], own_diag * v[0][1][:24]) for v in vectors[:4]]
+        def krylov(depth, force, both, cuts=None):
+            moved = [move(depth) for move in moves]
+            faces = [[jnp.minimum(depth[t], m[t]) for m in moved] for t in range(2)]
+            if cuts is not None:
+                faces = [[e, w, n * cuts[0], s * cuts[1]] for e, w, n, s in faces]
+            diag = [2.0 + ((faces[t][0] + faces[t][1]) + (faces[t][2] + faces[t][3])) for t in range(2)]
+            inverse = [1.0 / diag[t] for t in range(2)]
+
+            def over_diag(hi, lo, t):
+                q, _ = short(hi * inverse[t], 0.0)
+                return q, ((hi - diag[t] * q) + lo) * inverse[t]
+
+            vectors = [[short(*over_diag(force[t], 0.0, t)) for t in range(2)]]
+            for k in range(4):
+                last = vectors[-1]
+                high = [move((last[0][0], last[1][0])) for move in moves]
+                low = [move((last[0][1], last[1][1])) for move in moves]
+                following = []
+                for t in range(2 if both or k < 3 else 1):
+                    terms = [faces[t][i] * high[i][t] for i in range(4)]
+                    fine = [faces[t][i] * low[i][t] for i in range(4)]
+                    s0, e0 = two_sum(terms[0], terms[1])
+                    s1, e1 = two_sum(terms[2], terms[3])
+                    s, e2 = two_sum(s0, s1)
+                    rest = ((e0 + e1) + e2) + ((fine[0] + fine[1]) + (fine[2] + fine[3]))
+                    q, q_low = over_diag(s, rest, t)
+                    s, e = two_sum(last[t][0], -q)
+                    following.append(short(s, e + (last[t][1] - q_low)))
+                vectors.append(following)
+            return diag, vectors
+
+        def counted(pair):
+            cells = jnp.where(lane40 < 128 - HALO, pair[0], pair[1])
+            first = jnp.where(sub < HALO, cells[24:32], cells[0:8])
+            return jnp.concatenate([first, cells[8:24]], 0)
+
+        row40 = iota((40, 128), 0)
+        cuts = [jnp.where(row40 == row, has_north, 1.0) for row in (23, 24)]
+        diag, vectors = krylov(ahead(0), ahead(1), True, cuts)
+        terms = [tuple(counted((v[0][i], v[1][i])) for i in range(2)) for v in vectors]
+        scale = counted(diag)
+        weighted = [quick(scale * hi, scale * lo) for hi, lo in terms[:4]]
+        terms = [quick(hi, lo) for hi, lo in terms]
 
         sums = []
         for n in range(8):
-            product = dd_mul(weighted[n // 2], own_vectors[n - n // 2])
+            product = dd_mul(weighted[n // 2], terms[n - n // 2])
             tiles = [(product[0][8 * i:8 * i + 8], product[1][8 * i:8 * i + 8]) for i in range(3)]
             sums.append(dd_add(dd_add(tiles[0], tiles[1]), tiles[2]))
 
@@ -377,6 +387,14 @@
         pl.semaphore_wait(ready, len(relay))
         for j, peer in enumerate(plane_peer):
             remote(partial, gather_a.at[j], 5, peer).start()
+        surf_copy(NE, (2, 1), surf_b.at[pl.ds(5, 1)], 8).start()
+        surf_copy(NW, (2, 1), surf_b.at[pl.ds(4, 1)], 8).start()
+        surf_copy(SW, (0, 1), surf_b.at[pl.ds(3, 1)], 8).start()
+        surf_copy(W, (0, 3), surf_b.at[pl.ds(0, 3)], 8).start()
+        for d in (NE, NW, SE, SW):
+            corner_copy(d).start()
+        for d in (E, W):
+            edge_copy(d).start()
 
         def total(own, others, number):
             parts = [(own[0:1], own[1:2])] + [(others[j, 0:1], others[j, 1:2]) for j in range(number)]
@@ -386,8 +404,9 @@
             return parts[0]
 
         wait_all(recv_sem, 1)
-        count_own = jnp.concatenate([depth[0][:24], jnp.where(sub < 4, depth[0][24:32], depth[0][32:40])], 0)
-        count_side = jnp.concatenate([depth[1][:24], jnp.where(sub < 4, depth[1][24:32], depth[1][32:40])], 0)
+        wait_all(recv_sem, 7)
+        south_count, north_count = surf_s[0, 0] * has_south, surf_in[3, 0] * has_north
+        count_own = jnp.concatenate([surf[t, 0] for t in range(3)] + [jnp.where(sub < 4, north_count, south_count)], 0)
 
         def with_rows(f, block, north, south):
             up = pltpu.roll(north, (8 - 2 * f) % 8, 0) if f else north
@@ -415,17 +434,6 @@
         unrolled(lambda k, slot: main(k, slot, rows_a, 0), 0, half, UNROLL)
         unrolled(lambda k, slot: finish(k, 0), 0, half, FINISH)
 
-        lane32 = iota((32, 128), 1)
-
-        def spread(first, second):
-            x = jnp.where(lane32 < 8, jnp.where(lane32 < 4, pltpu.roll(first, 4, 1), pltpu.roll(second, 4, 1)), 0.0)
-            for step in (8, 16, 32, 64):
-                x = x + pltpu.roll(x, step, 1)
-            return x
-
-        counts[0] = spread(count_side, count_own)
-        counts[1] = spread(count_own, count_side)
-
         wait_all(recv_sem, 5)
         hi, lo = total(partial, gather_a, nplane - 1)
         mid[0:1] = hi
@@ -436,6 +444,23 @@
         wait_all(recv_sem, 2)
         unrolled(lambda k, slot: main(k, slot, rows_b, half), half, levels, UNROLL)
         unrolled(lambda k, slot: finish(k, half), half, levels, FINISH)
+        wait_all(recv_sem, 8)
+        depth = around_own(0)
+        diag, vectors = krylov(depth, around_own(1), False)
+        own_vectors = [quick(v[0][0][:24], v[0][1][:24]) for v in vectors]
+        own_diag = diag[0][:24]
+        count_side = jnp.concatenate([depth[1][:24], jnp.where(sub < 4, depth[1][24:32], depth[1][32:40])], 0)
+        lane32 = iota((32, 128), 1)
+
+        def spread(first, second):
+            x = jnp.where(lane32 < 8, jnp.where(lane32 < 4, pltpu.roll(first, 4, 1), pltpu.roll(second, 4, 1)), 0.0)
+            for step in (8, 16, 32, 64):
+                x = x + pltpu.roll(x, step, 1)
+            return x
+
+        counts[0] = spread(count_side, count_own)
+        counts[1] = spread(count_own, count_side)
+
         wait_all(recv_sem, 3)
         wait_all(recv_sem, 4)
         left24, left8 = lane24 % 8 < 4, lane % 8 < 4
@@ -504,13 +529,14 @@
             d = own_diag[rows]
             r_ref[rows] = (d * rest[0] + d * rest[1]) * (1.0 / 65536.0)
 
-        for i in range(7):
+        for i in range(9):
             wait_all(send_sem, i)
 
     scratch = [
         pltpu.VMEM((24, 128), F32), pltpu.VMEM((24, 128), jnp.int32), pltpu.VMEM((24, 128), jnp.int32),
         pltpu.VMEM((4, levels, 24, 128), F32),
-        pltpu.VMEM((3, 2, 8, 128), F32), pltpu.VMEM((12, 2, 8, 128), F32),
+        pltpu.VMEM((3, 2, 8, 128), F32), pltpu.VMEM((7, 2, 8, 128), F32),
+        pltpu.VMEM((1, 2, 8, 128), F32), pltpu.VMEM((6, 2, 8, 128), F32),
         pltpu.VMEM((4, groups, 24, 128), F32), pltpu.VMEM((2, 4, groups, 24, 128), F32),
         pltpu.VMEM((entries, 8, 128), F32), pltpu.VMEM((entries, 8, 128), F32),
         pltpu.VMEM((2, half, 8, 128), F32), pltpu.VMEM((2, entries - half, 8, 128), F32),
@@ -520,7 +546,7 @@
         pltpu.VMEM((4, groups, 24, 128), F32),
         pltpu.VMEM((2, 128), F32), pltpu.VMEM((nplane - 1, 2, 128), F32),
         pltpu.VMEM((2, 128), F32), pltpu.VMEM((nline - 1, 2, 128), F32),
-        pltpu.SemaphoreType.DMA((5,)), pltpu.SemaphoreType.DMA((7,)), pltpu.SemaphoreType.DMA((7,)),
+        pltpu.SemaphoreType.DMA((5,)), pltpu.SemaphoreType.DMA((9,)), pltpu.SemaphoreType.DMA((9,)),
         pltpu.SemaphoreType.REGULAR,
     ]
     return kernel, scratch

time: 27.1 us -> 25.7 us (0.948)
  Pallas kernels: 26.3 us -> 24.9 us
    pallas_call x1, Pallas kernels: 25 us -> 23.6 us  [per_device(): pl.pallas_call(kernel, out_shape=(pltpu.VMEM(surface_forcing.shape, F32),...]
where the time goes in v4:
time: 25.7 us; the launch traced here: 25.6 us
  Pallas kernels  24.9 us (97%)
  between operations  0.64 us (2%)
    pallas_call x1, Pallas kernels, per_device(): pl.pallas_call(kernel, out_shape=(pltpu.VMEM(surface_forcing.shape, F32),...  23.6 us
    pallas_call x1, Pallas kernels, per_device(): pl.pallas_call(hand_out, out_shape=tuple((jax.ShapeDtypeStruct(r.shape, F...  1.32 us

profile of v4, /device:TPU:1, one launch (start us, length us, event | category | flops | bytes accessed | tf_op | source)
XLA Modules:
  0.0 25.6 jit_solution(17498496566433642709)
XLA Ops:
  0.6 23.6 %ocean.1 = (f32[24,128]{1,0:T(8,128)S(1)}, f32[24,128]{1,0:T(8,128)S(1)}, f32[4,40,24,128]{3,2,1,0:T(8,128)S(1)}) custom-call(f32[24,128]{1,0:T(8,128)} %forcing_hbm.1, s32[24,128]{1,0:T(8,128)} %sea_hbm.1, s32[24,128]{1,0:T(8,128)} %count_hbm.1, f32[4,40,24,128]{3,2,1,0:T(8,128)} %state_hbm.1), custom_call_target="tpu_custom_call" | custom-call | tf_op jit(solution)/shard_map/ocean/pallas_call | solution.py:573
  24.3 1.3 %hand_out.1 = (f32[24,128]{1,0:T(8,128)}, f32[24,128]{1,0:T(8,128)}, f32[4,40,24,128]{3,2,1,0:T(8,128)}) custom-call(f32[24,128]{1,0:T(8,128)S(1)} %get-tuple-element.6.x_ref, f32[24,128]{1,0:T(8,128)S(1)} %get-tuple-element.7.r_ref, f32[4,40,24,128]{3,2,1,0:T(8,128)S(1)} %get-tuple-element.8.tend_ref), custom_call_target="tpu_custom_call" | custom-call | tf_op jit(solution)/shard_map/hand_out/pallas_call | solution.py:590

commit v5 on v4

--- a/solution.py
+++ b/solution.py
@@ -13,7 +13,7 @@
 VISC = 0.02
 HALO = 5
 UNROLL = 2
-FINISH = 8
+FINISH = 4
 DIRS = ((1, 0), (-1, 0), (0, 1), (0, -1), (1, 1), (-1, -1), (1, -1), (-1, 1))
 OPP = (1, 0, 3, 2, 5, 4, 7, 6)
 E, W, N, S, NE, SW, SE, NW = range(8)
@@ -56,18 +56,18 @@
 
 def dd_mul(a, b):
     p, e = two_prod(a[0], b[0])
-    return quick(p, e + (a[0] * b[1] + a[1] * b[0]))
+    return p, e + (a[0] * b[1] + a[1] * b[0])
 
 
 def dd_neg(a):
     return -a[0], -a[1]
 
 
-def dd_inverse(b):
-    r = 1.0 / b[0]
-    p, e = two_prod(r, b[0])
-    rest = ((1.0 - p) - e) - r * b[1]
-    return quick(r, rest * r)
+def dd_div(a, b, r):
+    q = a[0] * r
+    p, e = two_prod(q, b[0])
+    rest = ((a[0] - p) - e) + (a[1] - q * b[1])
+    return q, rest * r
 
 
 def iota(shape, dim):
@@ -88,8 +88,8 @@
     p, q = [one], [one]
     x = []
     for k in range(4):
-        inverse = dd_inverse(t[k + 1])
-        alpha = dd_mul(s[k], inverse)
+        inverse = 1.0 / t[k + 1][0]
+        alpha = dd_div(s[k], t[k + 1], inverse)
         minus = dd_neg(alpha)
         x = [dd_add(x[i], dd_mul(alpha, q[i])) if i < len(x) else dd_mul(alpha, q[i]) for i in range(k + 1)]
         moved = [dd_mul(minus, c) for c in q]
@@ -97,7 +97,7 @@
         if k < 3:
             last = 6 - k
             s_next = {j: dd_add(s[j], dd_mul(minus, t[j + 1])) for j in range(k + 1, last + 1)}
-            beta = dd_mul(dd_neg(s_next[k + 1]), inverse)
+            beta = dd_div(dd_neg(s_next[k + 1]), t[k + 1], inverse)
             t = {j: dd_add(s_next[j], dd_mul(beta, t[j])) for j in range(k + 2, last + 1)}
             s = s_next
             q = [dd_add(p[i], dd_mul(beta, q[i])) if i <= k else p[i] for i in range(k + 2)]
@@ -145,11 +145,11 @@
 def make_kernel(nx, ny, nlat, levels):
     nplane = nx * ny
     nline = CORES * nlat
-    half = 3 * levels // 5
+    half = 7 * levels // 10
     groups = -(-levels // GROUP)
     entries = levels + groups
     def kernel(forcing_hbm, sea_hbm, count_hbm, state_hbm, x_ref, r_ref, tend,
-               forcing, sea, count, state, surf, surf_in, surf_s, surf_b, edges, edges_in, rows_up, rows_down,
+               forcing, sea, count, state, surf, surf_in, surf_s, surf_b, surf_n, edges, edges_in, rows_up, rows_down,
                rows_a, rows_b, corners_in, counts, masked, laps, weight, edge_out, partial, gather_a, mid, gather_b, in_sem, send_sem, recv_sem, ready):
         x, y = lax.axis_index("x"), lax.axis_index("y")
         core, lat = lax.axis_index("core"), lax.axis_index("lat")
@@ -226,14 +226,23 @@
         def edge_copy(d):
             return remote(edges, edges_in.at[OPP[d]], 4, near[d])
 
-        landing = (surf_in, rows_a, rows_b, corners_in, edges_in, gather_a, gather_b, surf_s, surf_b)
+        landing = (surf_in, rows_a, rows_b, corners_in, edges_in, gather_a, gather_b, surf_s, surf_b, surf_n)
 
         def wait_all(sem, i):
             pltpu.make_async_copy(landing[i], landing[i], sem.at[i]).wait()
 
-        surf_copy(SE, (0, 2), surf_in.at[pl.ds(5, 2)], 0).start()
-        surf_copy(E, (0, 3), surf_in.at[pl.ds(0, 3)], 0).start()
-        surf_copy(S, (0, 2), surf_in.at[pl.ds(3, 2)], 0).start()
+        southward = (surf_copy(SE, (0, 2), surf_n.at[pl.ds(2, 2)], 9), surf_copy(S, (0, 2), surf_n.at[pl.ds(0, 2)], 9))
+
+        @pl.when(lat > 0)
+        def _():
+            southward[0].start()
+
+        surf_copy(E, (0, 3), surf_in, 0).start()
+
+        @pl.when(lat > 0)
+        def _():
+            southward[1].start()
+
         surf_copy(N, (2, 1), surf_s, 7).start()
         for peer in relay:
             pl.semaphore_signal(ready, inc=1, device_id=peer, device_id_type=MESH)
@@ -277,22 +286,27 @@
             rows_up[levels + g] = up
             rows_down[levels + g] = down
 
-        for d in (N, S):
-            rows_copy(d, 1).start()
         wait_all(recv_sem, 0)
 
-        has_north = jnp.where(lat < nlat - 1, 1.0, 0.0).astype(F32)
+        @pl.when(lat < nlat - 1)
+        def _():
+            wait_all(recv_sem, 9)
+
+
         has_south = jnp.where(lat > 0, 1.0, 0.0).astype(F32)
 
+        def from_north(tile, v):
+            return jnp.where(lat < nlat - 1, surf_n[tile, v], 0.0)
+
         def ahead(v):
-            own = [surf[t, v] for t in range(3)] + [surf_in[3 + t, v] for t in range(2)]
-            west = [surf_in[t, v] for t in range(3)] + [surf_in[5 + t, v] for t in range(2)]
+            own = [surf[t, v] for t in range(3)] + [from_north(t, v) for t in range(2)]
+            west = [surf_in[t, v] for t in range(3)] + [from_north(2 + t, v) for t in range(2)]
             return jnp.concatenate(own, 0), jnp.concatenate(west, 0)
 
         def around_own(v):
-            own = [surf[t, v] for t in range(3)] + [surf_in[3, v] * has_north, surf_s[0, v] * has_south]
+            own = [surf[t, v] for t in range(3)] + [from_north(0, v), surf_s[0, v] * has_south]
             side = [jnp.where(lane < 64, surf_b[t, v], surf_in[t, v]) for t in range(3)]
-            side.append(jnp.where(lane < 64, surf_b[3, v], surf_in[5, v]) * has_north)
+            side.append(jnp.where(lane < 64, jnp.where(lat < nlat - 1, surf_b[3, v], 0.0), from_north(2, v)))
             side.append(jnp.where(lane < 64, surf_b[4, v], surf_b[5, v]) * has_south)
             return jnp.concatenate(own, 0), jnp.concatenate(side, 0)
 
@@ -300,11 +314,13 @@
 
         def to_east(pair):
             a, b = shift_lanes(pair[0], 1), shift_lanes(pair[1], 1)
-            return jnp.where(lane40 == 127, b, a), jnp.where(lane40 == 127, a, b)
+            last = iota(a.shape, 1) == 127
+            return jnp.where(last, b, a), jnp.where(last, a, b)
 
         def to_west(pair):
             a, b = shift_lanes(pair[0], -1), shift_lanes(pair[1], -1)
-            return jnp.where(lane40 == 0, b, a), jnp.where(lane40 == 0, a, b)
+            first = iota(a.shape, 1) == 0
+            return jnp.where(first, b, a), jnp.where(first, a, b)
 
         def to_north(pair):
             return shift_rows(pair[0], 1), shift_rows(pair[1], 1)
@@ -313,11 +329,11 @@
             return shift_rows(pair[0], -1), shift_rows(pair[1], -1)
 
         moves = (to_east, to_west, to_north, to_south)
-        def krylov(depth, force, both, cuts=None):
+        def krylov(depth, force, both, cut=None, kept=40):
             moved = [move(depth) for move in moves]
             faces = [[jnp.minimum(depth[t], m[t]) for m in moved] for t in range(2)]
-            if cuts is not None:
-                faces = [[e, w, n * cuts[0], s * cuts[1]] for e, w, n, s in faces]
+            if cut is not None:
+                faces = [[e, w, n, s * cut] for e, w, n, s in faces]
             diag = [2.0 + ((faces[t][0] + faces[t][1]) + (faces[t][2] + faces[t][3])) for t in range(2)]
             inverse = [1.0 / diag[t] for t in range(2)]
 
@@ -330,6 +346,11 @@
                 last = vectors[-1]
                 high = [move((last[0][0], last[1][0])) for move in moves]
                 low = [move((last[0][1], last[1][1])) for move in moves]
+                if k == 0 and kept < 40:
+                    high, low = ([[x[:kept] for x in pair] for pair in part] for part in (high, low))
+                    last = [tuple(x[:kept] for x in pair) for pair in last]
+                    faces = [[x[:kept] for x in part] for part in faces]
+                    diag, inverse = [x[:kept] for x in diag], [x[:kept] for x in inverse]
                 following = []
                 for t in range(2 if both or k < 3 else 1):
                     terms = [faces[t][i] * high[i][t] for i in range(4)]
@@ -345,13 +366,13 @@
             return diag, vectors
 
         def counted(pair):
-            cells = jnp.where(lane40 < 128 - HALO, pair[0], pair[1])
+            cells = jnp.where(iota(pair[0].shape, 1) < 128 - HALO, pair[0], pair[1])
             first = jnp.where(sub < HALO, cells[24:32], cells[0:8])
-            return jnp.concatenate([first, cells[8:24]], 0)
-
-        row40 = iota((40, 128), 0)
-        cuts = [jnp.where(row40 == row, has_north, 1.0) for row in (23, 24)]
-        diag, vectors = krylov(ahead(0), ahead(1), True, cuts)
+            return jnp.concatenate([first, cells[8:24], jnp.where(sub < southern, cells[0:8], 0.0)], 0)
+
+        southern = jnp.where(lat > 0, 0, HALO)
+        cut = jnp.where(iota((40, 128), 0) == 0, has_south, 1.0)
+        diag, vectors = krylov(ahead(0), ahead(1), True, cut, 32)
         terms = [tuple(counted((v[0][i], v[1][i])) for i in range(2)) for v in vectors]
         scale = counted(diag)
         weighted = [quick(scale * hi, scale * lo) for hi, lo in terms[:4]]
@@ -360,8 +381,8 @@
         sums = []
         for n in range(8):
             product = dd_mul(weighted[n // 2], terms[n - n // 2])
-            tiles = [(product[0][8 * i:8 * i + 8], product[1][8 * i:8 * i + 8]) for i in range(3)]
-            sums.append(dd_add(dd_add(tiles[0], tiles[1]), tiles[2]))
+            tiles = [(product[0][8 * i:8 * i + 8], product[1][8 * i:8 * i + 8]) for i in range(4)]
+            sums.append(dd_add(dd_add(tiles[0], tiles[1]), dd_add(tiles[2], tiles[3])))
 
         def fold(a, b, near_mask, step):
             def one(i):
@@ -385,8 +406,10 @@
         partial[1:2, 0:8] = level[1]
 
         pl.semaphore_wait(ready, len(relay))
-        for j, peer in enumerate(plane_peer):
+        for j, peer in enumerate(line_peer):
             remote(partial, gather_a.at[j], 5, peer).start()
+        for d in (N, S):
+            rows_copy(d, 1).start()
         surf_copy(NE, (2, 1), surf_b.at[pl.ds(5, 1)], 8).start()
         surf_copy(NW, (2, 1), surf_b.at[pl.ds(4, 1)], 8).start()
         surf_copy(SW, (0, 1), surf_b.at[pl.ds(3, 1)], 8).start()
@@ -405,7 +428,7 @@
 
         wait_all(recv_sem, 1)
         wait_all(recv_sem, 7)
-        south_count, north_count = surf_s[0, 0] * has_south, surf_in[3, 0] * has_north
+        south_count, north_count = surf_s[0, 0] * has_south, from_north(0, 0)
         count_own = jnp.concatenate([surf[t, 0] for t in range(3)] + [jnp.where(sub < 4, north_count, south_count)], 0)
 
         def with_rows(f, block, north, south):
@@ -435,10 +458,10 @@
         unrolled(lambda k, slot: finish(k, 0), 0, half, FINISH)
 
         wait_all(recv_sem, 5)
-        hi, lo = total(partial, gather_a, nplane - 1)
+        hi, lo = total(partial, gather_a, nline - 1)
         mid[0:1] = hi
         mid[1:2] = lo
-        for j, peer in enumerate(line_peer):
+        for j, peer in enumerate(plane_peer):
             remote(mid, gather_b.at[j], 6, peer).start()
 
         wait_all(recv_sem, 2)
@@ -499,10 +522,10 @@
         for k in range(levels):
             g, back = k // GROUP, (252 - 8 * (k % GROUP)) % 128
             for f in range(4):
-                tend[f, k] = jnp.where(rim, pltpu.roll(edge_out[f, g], back, 1), tend[f, k])
+                pltpu.store(tend.at[f, k], pltpu.roll(edge_out[f, g], back, 1), mask=rim)
 
         wait_all(recv_sem, 6)
-        level = total(mid, gather_b, nline - 1)
+        level = total(mid, gather_b, nplane - 1)
 
         def scalar(a, n):
             return jnp.broadcast_to(a[0:1, n:n + 1], (8, 128))
@@ -532,11 +555,16 @@
         for i in range(9):
             wait_all(send_sem, i)
 
+        @pl.when(lat > 0)
+        def _():
+            wait_all(send_sem, 9)
+
+
     scratch = [
         pltpu.VMEM((24, 128), F32), pltpu.VMEM((24, 128), jnp.int32), pltpu.VMEM((24, 128), jnp.int32),
         pltpu.VMEM((4, levels, 24, 128), F32),
-        pltpu.VMEM((3, 2, 8, 128), F32), pltpu.VMEM((7, 2, 8, 128), F32),
-        pltpu.VMEM((1, 2, 8, 128), F32), pltpu.VMEM((6, 2, 8, 128), F32),
+        pltpu.VMEM((3, 2, 8, 128), F32), pltpu.VMEM((3, 2, 8, 128), F32),
+        pltpu.VMEM((1, 2, 8, 128), F32), pltpu.VMEM((6, 2, 8, 128), F32), pltpu.VMEM((4, 2, 8, 128), F32),
         pltpu.VMEM((4, groups, 24, 128), F32), pltpu.VMEM((2, 4, groups, 24, 128), F32),
         pltpu.VMEM((entries, 8, 128), F32), pltpu.VMEM((entries, 8, 128), F32),
         pltpu.VMEM((2, half, 8, 128), F32), pltpu.VMEM((2, entries - half, 8, 128), F32),
@@ -544,9 +572,9 @@
         pltpu.VMEM((2, 32, 128), F32), pltpu.VMEM((UNROLL, 4, 48, 128), F32),
         pltpu.VMEM((half, 4, 40, 128), F32), pltpu.VMEM((half, 24, 128), F32),
         pltpu.VMEM((4, groups, 24, 128), F32),
+        pltpu.VMEM((2, 128), F32), pltpu.VMEM((nline - 1, 2, 128), F32),
         pltpu.VMEM((2, 128), F32), pltpu.VMEM((nplane - 1, 2, 128), F32),
-        pltpu.VMEM((2, 128), F32), pltpu.VMEM((nline - 1, 2, 128), F32),
-        pltpu.SemaphoreType.DMA((5,)), pltpu.SemaphoreType.DMA((9,)), pltpu.SemaphoreType.DMA((9,)),
+        pltpu.SemaphoreType.DMA((5,)), pltpu.SemaphoreType.DMA((10,)), pltpu.SemaphoreType.DMA((10,)),
         pltpu.SemaphoreType.REGULAR,
     ]
     return kernel, scratch

time: 25.7 us -> 25.3 us (0.984)
  Pallas kernels: 24.9 us -> 24.5 us
    pallas_call x1, Pallas kernels: 23.6 us -> 23.2 us  [per_device(): pl.pallas_call(kernel, out_shape=(pltpu.VMEM(surface_forcing.shape, F32),...]
where the time goes in v5:
time: 25.3 us; the launch traced here: 25.1 us
  Pallas kernels  24.5 us (97%)
  between operations  0.64 us (3%)
    pallas_call x1, Pallas kernels, per_device(): pl.pallas_call(kernel, out_shape=(pltpu.VMEM(surface_forcing.shape, F32),...  23.2 us
    pallas_call x1, Pallas kernels, per_device(): pl.pallas_call(hand_out, out_shape=tuple((jax.ShapeDtypeStruct(r.shape, F...  1.32 us

profile of v5, /device:TPU:1, one launch (start us, length us, event | category | flops | bytes accessed | tf_op | source)
XLA Modules:
  0.0 25.1 jit_solution(13656583080497236895)
XLA Ops:
  0.6 23.2 %ocean.1 = (f32[24,128]{1,0:T(8,128)S(1)}, f32[24,128]{1,0:T(8,128)S(1)}, f32[4,40,24,128]{3,2,1,0:T(8,128)S(1)}) custom-call(f32[24,128]{1,0:T(8,128)} %forcing_hbm.1, s32[24,128]{1,0:T(8,128)} %sea_hbm.1, s32[24,128]{1,0:T(8,128)} %count_hbm.1, f32[4,40,24,128]{3,2,1,0:T(8,128)} %state_hbm.1), custom_call_target="tpu_custom_call" | custom-call | tf_op jit(solution)/shard_map/ocean/pallas_call | solution.py:601
  23.8 1.3 %hand_out.1 = (f32[24,128]{1,0:T(8,128)}, f32[24,128]{1,0:T(8,128)}, f32[4,40,24,128]{3,2,1,0:T(8,128)}) custom-call(f32[24,128]{1,0:T(8,128)S(1)} %get-tuple-element.6.x_ref, f32[24,128]{1,0:T(8,128)S(1)} %get-tuple-element.7.r_ref, f32[4,40,24,128]{3,2,1,0:T(8,128)S(1)} %get-tuple-element.8.tend_ref), custom_call_target="tpu_custom_call" | custom-call | tf_op jit(solution)/shard_map/hand_out/pallas_call | solution.py:618

commit v6 on v5

--- a/solution.py
+++ b/solution.py
@@ -145,12 +145,13 @@
 def make_kernel(nx, ny, nlat, levels):
     nplane = nx * ny
     nline = CORES * nlat
-    half = 7 * levels // 10
+    half = 4 * levels // 5
+    quarter = half // 4 * 2
     groups = -(-levels // GROUP)
     entries = levels + groups
     def kernel(forcing_hbm, sea_hbm, count_hbm, state_hbm, x_ref, r_ref, tend,
                forcing, sea, count, state, surf, surf_in, surf_s, surf_b, surf_n, edges, edges_in, rows_up, rows_down,
-               rows_a, rows_b, corners_in, counts, masked, laps, weight, edge_out, partial, gather_a, mid, gather_b, in_sem, send_sem, recv_sem, ready):
+               rows_a, rows_b, rows_c, corners_in, counts, masked, laps, weight, edge_out, partial, gather_a, mid, gather_b, in_sem, send_sem, recv_sem, ready):
         x, y = lax.axis_index("x"), lax.axis_index("y")
         core, lat = lax.axis_index("core"), lax.axis_index("lat")
 
@@ -216,8 +217,9 @@
 
         def rows_copy(d, part):
             source = rows_up if DIRS[d][1] > 0 else rows_down
-            span = pl.ds(0, half) if part == 0 else pl.ds(half, entries - half)
-            return remote(source.at[span], (rows_a, rows_b)[part].at[OPP[d] - 2], 1 + part, near[d])
+            span = (pl.ds(0, quarter), pl.ds(half, entries - half), pl.ds(quarter, half - quarter))[part]
+            target = (rows_a, rows_b, rows_c)[part].at[OPP[d] - 2]
+            return remote(source.at[span], target, (1, 2, 10)[part], near[d])
 
         def corner_copy(d):
             source = rows_up if DIRS[d][1] > 0 else rows_down
@@ -226,7 +228,7 @@
         def edge_copy(d):
             return remote(edges, edges_in.at[OPP[d]], 4, near[d])
 
-        landing = (surf_in, rows_a, rows_b, corners_in, edges_in, gather_a, gather_b, surf_s, surf_b, surf_n)
+        landing = (surf_in, rows_a, rows_b, corners_in, edges_in, gather_a, gather_b, surf_s, surf_b, surf_n, rows_c)
 
         def wait_all(sem, i):
             pltpu.make_async_copy(landing[i], landing[i], sem.at[i]).wait()
@@ -278,8 +280,9 @@
             return carry
 
         lax.fori_loop(0, levels, pack_rows, 0)
-        for d in (N, S):
-            rows_copy(d, 0).start()
+        for part in (0, 2):
+            for d in (N, S):
+                rows_copy(d, part).start()
         lax.fori_loop(0, 4, pack_edges, 0)
         for g in range(groups):
             up, down = packed_rows(lambda f, rows: edges[f, g, rows])
@@ -436,9 +439,9 @@
             down = pltpu.roll(south, 6 - 2 * f, 0) if f < 3 else south
             return jnp.concatenate([block, jnp.where(sub < 4, up, down)], 0)
 
-        def main(k, slot, rows_in, base):
+        def main(k, slot, rows_in, first, base):
             active = jnp.where(count_own > k.astype(F32), 1.0, 0.0)
-            north, south = rows_in[N - 2, k - base], rows_in[S - 2, k - base]
+            north, south = rows_in[N - 2, k - first], rows_in[S - 2, k - first]
             quads = [with_rows(f, state[f, k], north, south) for f in range(4)]
             for f, value in enumerate(first_pass(active, quads, masked.at[slot], laps.at[k - base], weight.at[k - base])):
                 tend[f, k] = value
@@ -454,7 +457,9 @@
                 return carry
             lax.fori_loop(0, (last - first) // by, step, 0)
 
-        unrolled(lambda k, slot: main(k, slot, rows_a, 0), 0, half, UNROLL)
+        unrolled(lambda k, slot: main(k, slot, rows_a, 0, 0), 0, quarter, UNROLL)
+        wait_all(recv_sem, 10)
+        unrolled(lambda k, slot: main(k, slot, rows_c, quarter, 0), quarter, half, UNROLL)
         unrolled(lambda k, slot: finish(k, 0), 0, half, FINISH)
 
         wait_all(recv_sem, 5)
@@ -465,7 +470,7 @@
             remote(mid, gather_b.at[j], 6, peer).start()
 
         wait_all(recv_sem, 2)
-        unrolled(lambda k, slot: main(k, slot, rows_b, half), half, levels, UNROLL)
+        unrolled(lambda k, slot: main(k, slot, rows_b, half, half), half, levels, UNROLL)
         unrolled(lambda k, slot: finish(k, half), half, levels, FINISH)
         wait_all(recv_sem, 8)
         depth = around_own(0)
@@ -552,7 +557,7 @@
             d = own_diag[rows]
             r_ref[rows] = (d * rest[0] + d * rest[1]) * (1.0 / 65536.0)
 
-        for i in range(9):
+        for i in (0, 1, 2, 3, 4, 5, 6, 7, 8, 10):
             wait_all(send_sem, i)
 
         @pl.when(lat > 0)
@@ -567,14 +572,15 @@
         pltpu.VMEM((1, 2, 8, 128), F32), pltpu.VMEM((6, 2, 8, 128), F32), pltpu.VMEM((4, 2, 8, 128), F32),
         pltpu.VMEM((4, groups, 24, 128), F32), pltpu.VMEM((2, 4, groups, 24, 128), F32),
         pltpu.VMEM((entries, 8, 128), F32), pltpu.VMEM((entries, 8, 128), F32),
-        pltpu.VMEM((2, half, 8, 128), F32), pltpu.VMEM((2, entries - half, 8, 128), F32),
+        pltpu.VMEM((2, quarter, 8, 128), F32), pltpu.VMEM((2, entries - half, 8, 128), F32),
+        pltpu.VMEM((2, half - quarter, 8, 128), F32),
         pltpu.VMEM((4, groups, 8, 128), F32),
         pltpu.VMEM((2, 32, 128), F32), pltpu.VMEM((UNROLL, 4, 48, 128), F32),
         pltpu.VMEM((half, 4, 40, 128), F32), pltpu.VMEM((half, 24, 128), F32),
         pltpu.VMEM((4, groups, 24, 128), F32),
         pltpu.VMEM((2, 128), F32), pltpu.VMEM((nline - 1, 2, 128), F32),
         pltpu.VMEM((2, 128), F32), pltpu.VMEM((nplane - 1, 2, 128), F32),
-        pltpu.SemaphoreType.DMA((5,)), pltpu.SemaphoreType.DMA((10,)), pltpu.SemaphoreType.DMA((10,)),
+        pltpu.SemaphoreType.DMA((5,)), pltpu.SemaphoreType.DMA((11,)), pltpu.SemaphoreType.DMA((11,)),
         pltpu.SemaphoreType.REGULAR,
     ]
     return kernel, scratch

time: 25.3 us -> 24.8 us (0.980)
  Pallas kernels: 24.5 us -> 24 us
    pallas_call x1, Pallas kernels: 23.2 us -> 22.7 us  [per_device(): pl.pallas_call(kernel, out_shape=(pltpu.VMEM(surface_forcing.shape, F32),...]
where the time goes in v6:
time: 24.8 us; the launch traced here: 24.7 us
  Pallas kernels  24 us (97%)
  between operations  0.64 us (3%)
    pallas_call x1, Pallas kernels, per_device(): pl.pallas_call(kernel, out_shape=(pltpu.VMEM(surface_forcing.shape, F32),...  22.7 us
    pallas_call x1, Pallas kernels, per_device(): pl.pallas_call(hand_out, out_shape=tuple((jax.ShapeDtypeStruct(r.shape, F...  1.32 us

profile of v6, /device:TPU:1, one launch (start us, length us, event | category | flops | bytes accessed | tf_op | source)
XLA Modules:
  0.0 24.7 jit_solution(14416648804961974787)
XLA Ops:
  0.6 22.7 %ocean.1 = (f32[24,128]{1,0:T(8,128)S(1)}, f32[24,128]{1,0:T(8,128)S(1)}, f32[4,40,24,128]{3,2,1,0:T(8,128)S(1)}) custom-call(f32[24,128]{1,0:T(8,128)} %forcing_hbm.1, s32[24,128]{1,0:T(8,128)} %sea_hbm.1, s32[24,128]{1,0:T(8,128)} %count_hbm.1, f32[4,40,24,128]{3,2,1,0:T(8,128)} %state_hbm.1), custom_call_target="tpu_custom_call" | custom-call | tf_op jit(solution)/shard_map/ocean/pallas_call | solution.py:607
  23.3 1.3 %hand_out.1 = (f32[24,128]{1,0:T(8,128)}, f32[24,128]{1,0:T(8,128)}, f32[4,40,24,128]{3,2,1,0:T(8,128)}) custom-call(f32[24,128]{1,0:T(8,128)S(1)} %get-tuple-element.6.x_ref, f32[24,128]{1,0:T(8,128)S(1)} %get-tuple-element.7.r_ref, f32[4,40,24,128]{3,2,1,0:T(8,128)S(1)} %get-tuple-element.8.tend_ref), custom_call_target="tpu_custom_call" | custom-call | tf_op jit(solution)/shard_map/hand_out/pallas_call | solution.py:624

commit v7 on v6

--- a/solution.py
+++ b/solution.py
@@ -13,7 +13,7 @@
 VISC = 0.02
 HALO = 5
 UNROLL = 2
-FINISH = 4
+FINISH = 8
 DIRS = ((1, 0), (-1, 0), (0, 1), (0, -1), (1, 1), (-1, -1), (1, -1), (-1, 1))
 OPP = (1, 0, 3, 2, 5, 4, 7, 6)
 E, W, N, S, NE, SW, SE, NW = range(8)

time: 24.8 us -> 24.8 us (level)
  no operation moved by 1% of the time
where the time goes in v7:
time: 24.8 us; the launch traced here: 24.6 us
  Pallas kernels  24 us (97%)
  between operations  0.64 us (3%)
    pallas_call x1, Pallas kernels, per_device(): pl.pallas_call(kernel, out_shape=(pltpu.VMEM(surface_forcing.shape, F32),...  22.6 us
    pallas_call x1, Pallas kernels, per_device(): pl.pallas_call(hand_out, out_shape=tuple((jax.ShapeDtypeStruct(r.shape, F...  1.32 us

profile of v7, /device:TPU:1, one launch (start us, length us, event | category | flops | bytes accessed | tf_op | source)
XLA Modules:
  0.0 24.6 jit_solution(15025381995438881745)
XLA Ops:
  0.6 22.6 %ocean.1 = (f32[24,128]{1,0:T(8,128)S(1)}, f32[24,128]{1,0:T(8,128)S(1)}, f32[4,40,24,128]{3,2,1,0:T(8,128)S(1)}) custom-call(f32[24,128]{1,0:T(8,128)} %forcing_hbm.1, s32[24,128]{1,0:T(8,128)} %sea_hbm.1, s32[24,128]{1,0:T(8,128)} %count_hbm.1, f32[4,40,24,128]{3,2,1,0:T(8,128)} %state_hbm.1), custom_call_target="tpu_custom_call" | custom-call | tf_op jit(solution)/shard_map/ocean/pallas_call | solution.py:607
  23.3 1.3 %hand_out.1 = (f32[24,128]{1,0:T(8,128)}, f32[24,128]{1,0:T(8,128)}, f32[4,40,24,128]{3,2,1,0:T(8,128)}) custom-call(f32[24,128]{1,0:T(8,128)S(1)} %get-tuple-element.6.x_ref, f32[24,128]{1,0:T(8,128)S(1)} %get-tuple-element.7.r_ref, f32[4,40,24,128]{3,2,1,0:T(8,128)S(1)} %get-tuple-element.8.tend_ref), custom_call_target="tpu_custom_call" | custom-call | tf_op jit(solution)/shard_map/hand_out/pallas_call | solution.py:624
